TPU v7x, 256 devices: a whole 4x4x8 slice. The times are simulated.
256 devices in a mesh: lat: 8 (over x_lo, y), lon: 16 (over x_hi, z), lev: 2 (over core).
Axes of the slice: x: 4 (x_hi: 2, x_lo: 2; x = x_hi * 2 + x_lo), y: 4, z: 8, core: 2. Of those that a mesh axis runs over, the one named last changes fastest.
Arguments:
- increment: float32 [80, 128, 2048], P('lev', 'lat', 'lon'), may hold values from -6 to 6
- wind_u: float32 [80, 128, 2048], P('lev', 'lat', 'lon'), may hold values from -0.4 to 0.4
- wind_v: float32 [80, 128, 2048], P('lev', 'lat', 'lon'), may hold values from -0.4 to 0.4
- diffusion: float32 [80], P('lev'), may hold values from 0.02 to 0.2
- mixing: float32 [80, 80], P('lev'), may hold values from -0.15625 to 0.15625
- jacobian: bfloat16 [128, 80], P(None, 'lev'), may hold values from -0.625 to 0.625
- obs_weight: float32 [128], replicated, may hold values from 0.5 to 4
- innovation: bfloat16 [2, 8, 16, 16, 128, 128], P(None, 'lat', 'lon'), may hold values from -6 to 6
- counts: int32 [8, 16], P('lat', 'lon'), may hold values from 1 to 16, as said below
- column_lookup: int32 [8, 16, 2048], P('lat', 'lon'), may hold values from 0 to 2047, each once within a row
Outputs:
- gradient: float32 [80, 128, 2048], P('lev', 'lat', 'lon')
- cost: float32 [], replicated
Inputs may be any that keep to these rules, and one draw needn't show every extreme that they name: In every row of tiles with one latitude index the counts sum to 96, and the largest of them is 16.
All inputs are finite; a program needn't handle non-finite values.
Results may differ from a plain program's by a relative error of at most 0.005.
Values may be sent and summed in bfloat16 or wider, within the bound.
A program may use at most 64 MiB of HBM per device.

v0:
```python
import jax
import jax.numpy as jnp
from jax import lax
from jax.sharding import Mesh
from jax.sharding import PartitionSpec as P

LAT = ("lat_0", "lat_1")
LON = ("lon_0", "lon_1")
LAT_LON_LEV = ("lat_0", "lat_1", "lon_0", "lon_1", "lev")


def with_halo(shard, sides, width):
    edges = {}
    for axis, dim in sides:
        size, length = (lax.axis_size(axis), shard.shape[dim])
        up = [(i, (i + 1) % size) for i in range(size)]
        last = lax.slice_in_dim(shard, length - width, length, axis=dim)
        leading = lax.slice_in_dim(shard, 0, width, axis=dim)
        edges[dim] = (
            lax.ppermute(last, axis, up),
            lax.ppermute(leading, axis, [(b, a) for a, b in up]),
        )
    done = []
    for _, dim in sides:
        low, high = edges[dim]
        around = [(width, width) if d in done else (0, 0) for d in range(shard.ndim)]
        shard = jnp.concatenate([jnp.pad(low, around), shard, jnp.pad(high, around)], axis=dim)
        done.append(dim)
    return shard


def laid_out(pieces, dim):
    pieces = jnp.moveaxis(pieces, 0, dim)
    dims = pieces.shape
    return pieces.reshape(*dims[:dim], dims[dim] * dims[dim + 1], *dims[dim + 2 :])


def from_everyone(shard, axis):
    copies = jnp.broadcast_to(shard, (lax.axis_size(axis), *shard.shape))
    return lax.all_to_all(copies, axis, split_axis=0, concat_axis=0, tiled=True)


def gather_directly(shard, axis, dim):
    return laid_out(from_everyone(shard, axis), dim)


def over_axes(shard, axes):
    for axis in axes:
        shard = lax.psum(shard, axis)
    return shard


def neighbours(stacked):
    padded = with_halo(stacked.astype(jnp.bfloat16), ((LAT, 2), (LON, 3)), 1).astype(stacked.dtype)
    height = padded.shape[2]
    first_row = (lax.axis_index(LAT) == 0).astype(jnp.float32)
    final_row = (lax.axis_index(LAT) == lax.axis_size(LAT) - 1).astype(jnp.float32)
    rim_mask = (
        jnp.ones((height,), jnp.float32)
        .at[0]
        .set(1.0 - first_row)
        .at[height - 1]
        .set(1.0 - final_row)
    )
    padded = padded * rim_mask[None, None, :, None]
    northern = padded[:, :, 2:, 1:-1]
    southern = padded[:, :, :-2, 1:-1]
    eastern = padded[:, :, 1:-1, 2:]
    western = padded[:, :, 1:-1, :-2]
    return (northern, southern, eastern, western)


def horizontal(field, diffusion, wind_u, wind_v):
    northern, southern, eastern, western = neighbours(field[None])
    coefficient = diffusion[:, None, None]
    result = field + coefficient * (
        northern[0] + southern[0] + eastern[0] + western[0] - 4.0 * field
    )
    return (
        result
        - 0.5 * wind_u * (eastern[0] - western[0])
        - 0.5 * wind_v * (northern[0] - southern[0])
    )


def horizontal_back(adjoint, diffusion, wind_u, wind_v):
    stacked = jnp.stack([adjoint, 0.5 * wind_u * adjoint, 0.5 * wind_v * adjoint])
    northern, southern, eastern, western = neighbours(stacked)
    coefficient = diffusion[:, None, None]
    result = adjoint + coefficient * (
        northern[0] + southern[0] + eastern[0] + western[0] - 4.0 * adjoint
    )
    return result + (eastern[1] - western[1]) + (northern[2] - southern[2])


def vertical(smooth, mixing):
    flat = smooth.reshape(smooth.shape[0], -1)
    mixed = jnp.dot(
        mixing,
        lax.all_gather(flat.astype(jnp.bfloat16), "lev", axis=0, tiled=True).astype(jnp.float32),
        precision=lax.Precision.HIGHEST,
        preferred_element_type=jnp.float32,
    )
    return smooth + mixed.reshape(smooth.shape)


def vertical_back(adjoint, own_columns):
    flat = adjoint.reshape(adjoint.shape[0], -1)
    dispersed_blocks = lax.dot_general(
        own_columns,
        gather_directly(flat.astype(jnp.bfloat16), "lev", 0).astype(flat.dtype),
        (((0,), (0,)), ((), ())),
        precision=lax.Precision.HIGHEST,
        preferred_element_type=jnp.float32,
    )
    return adjoint + dispersed_blocks.reshape(adjoint.shape)


def take_profiles(state, columns, slot_count, block_width):
    level_count = state.shape[0]
    selected_columns = jnp.take(state.reshape(level_count, -1), columns, axis=1)
    return (
        selected_columns.reshape(level_count, slot_count, block_width)
        .astype(jnp.bfloat16)
        .transpose(1, 0, 2)
    )


def place_back(slots, inverse, shape):
    dispersed_blocks = slots.transpose(1, 0, 2).reshape(shape[0], -1).astype(jnp.float32)
    return jnp.take(dispersed_blocks, inverse, axis=1).reshape(shape)


def body(
    increment,
    wind_u,
    wind_v,
    diffusion,
    mixing,
    jacobian,
    obs_weight,
    innovation,
    counts,
    column_lookup,
):
    level_count = increment.shape[0]
    slot_count = column_lookup.shape[-1] // 128
    block_width = 128
    step_count = innovation.shape[0]
    channel_count = innovation.shape[-2]
    columns = column_lookup.reshape(-1)
    inverse = jnp.argsort(columns)
    live_float = (jnp.arange(slot_count) < counts.reshape(())).astype(jnp.float32)
    observed = innovation.reshape(step_count, slot_count, channel_count, block_width)
    own_columns = None
    all_rows = gather_directly(mixing, "lev", 0)
    own_columns = lax.dynamic_slice_in_dim(
        all_rows, lax.axis_index("lev") * level_count, level_count, 1
    )
    jac_full = gather_directly(jacobian, "lev", 1)
    state = increment
    forcings = []
    misfit_total = jnp.zeros((), jnp.float32)
    for step in range(step_count):
        state = vertical(horizontal(state, diffusion, wind_u, wind_v), mixing)
        profiles = take_profiles(state, columns, slot_count, block_width)
        full_profiles = gather_directly(profiles, "lev", 1)
        evolved = jnp.einsum(
            "nl,slc->snc", jac_full, full_profiles, preferred_element_type=jnp.float32
        )
        misfit = live_float[:, None, None] * (evolved - observed[step].astype(jnp.float32))
        scaled = obs_weight[None, :, None] * misfit
        misfit_total = misfit_total + jnp.sum(misfit * scaled)
        slots = jnp.einsum(
            "nl,snc->slc", jacobian, scaled.astype(jnp.bfloat16), preferred_element_type=jnp.float32
        )
        slots = slots.astype(jnp.bfloat16)
        forcings.append(place_back(slots, inverse, increment.shape))
    adjoint = jnp.zeros_like(increment)
    for step in range(step_count - 1, -1, -1):
        coupled = vertical_back(adjoint + forcings[step], own_columns)
        adjoint = horizontal_back(coupled, diffusion, wind_u, wind_v)
    gradient = increment + adjoint
    own_part = 0.5 * jnp.sum(increment * increment) + 0.5 * misfit_total / lax.axis_size("lev")
    total_cells = increment.size * lax.axis_size(LAT) * lax.axis_size(LON) * lax.axis_size("lev")
    cost = over_axes(own_part, LAT_LON_LEV) / total_cells
    return (gradient, cost)


def solution(mesh):
    split = Mesh(
        mesh.devices.reshape(2, 4, 2, 8, mesh.shape["lev"]),
        ("lat_0", "lat_1", "lon_0", "lon_1", "lev"),
    )
    in_specs = (
        P("lev", LAT, LON),
        P("lev", LAT, LON),
        P("lev", LAT, LON),
        P("lev"),
        P("lev", None),
        P(None, "lev"),
        P(),
        P(None, LAT, LON, None, None, None),
        P(LAT, LON),
        P(LAT, LON, None),
    )
    out_specs = (P("lev", LAT, LON), P())
    return jax.shard_map(body, mesh=split, in_specs=in_specs, out_specs=out_specs, check_vma=False)
```

profile of v0, /device:TPU:1, one launch (start us, length us, event | category | flops | bytes accessed | tf_op | source)
XLA Modules:
  0.0 190.3 jit_solution(2382379160425684982)
XLA Ops:
  1.9 8.9 %collective-permute-start.3 = (bf16[1,40,16,1]{3,1,2,0:T(8,128)(2,1)S(1)}, bf16[1,40,16,1]{3,1,2,0:T(8,128)(2,1)S(1)}, u32[]{:S(2)}, u32[]{:S(2)}) collective-permute-start(bf16[1,40,16,1]{3,1,2,0:T(8,128)(2,1)S(1)} %get-tuple-element.118), channel_id=1, source_target_pairs={{2,0},{4,2},{6,4},{8,6},{10,8},{12,10},{14,12},{16,14},{18,16},{20... | collective-permute-start | bytes 3848 | tf_op jit(solution)/shard_map/ppermute | solution.py:21
  10.8 2.8 %collective-permute-start.2 = (bf16[1,40,1,128]{3,1,2,0:T(8,128)(2,1)S(1)}, bf16[1,40,1,128]{3,1,2,0:T(8,128)(2,1)S(1)}, u32[]{:S(2)}, u32[]{:S(2)}) collective-permute-start(bf16[1,40,1,128]{3,1,2,0:T(8,128)(2,1)S(1)} %get-tuple-element.116), channel_id=1, source_target_pairs={{32,0},{64,32},{96,64},{128,96},{160,128},{192,160},{224,192},{0,2... | collective-permute-start | bytes 30728 | tf_op jit(solution)/shard_map/ppermute | solution.py:21
  13.6 1.3 broadcast_in_dim.22
  14.9 4.5 %all-to-all-start.1 = ((bf16[2,128,40]{1,2,0:T(8,128)(2,1)}), bf16[2,128,40]{1,2,0:T(8,128)(2,1)S(1)}, u32[]{:S(2)}, u32[]{:S(2)}) async-start(bf16[2,128,40]{1,2,0:T(8,128)(2,1)} %broadcast_in_dim.22), calls=%async_computation.1 | async-start | bytes 40960 | tf_op jit(solution)/shard_map/all_to_all | solution.py:40
  22.1 5.0 %sort.17 = (s32[2048]{0:T(1024)}, s32[2048]{0:T(1024)S(1)}) sort(s32[2048]{0:T(1024)S(1)} %bitcast.274, s32[2048]{0:T(1024)S(1)} %iota.10), dimensions={0}, to_apply=%region_0.2 | sort | flops 22528 | bytes 32768 | tf_op jit(solution)/shard_map/jit(argsort)/sort | solution.py:152
  28.7 2.0 %all_gather.6 = bf16[80,2048]{1,0:T(8,128)(2,1)S(1)} all-gather(bf16[40,2048]{1,0:T(8,128)(2,1)S(1)} %bitcast.267), channel_id=1, replica_groups=mesh['lat_0'=2,'lat_1'=4,'lon_0'=2,'lon_1'=8,'lev'=2] {'lev'}, dimensions={0}, use_global_device_ids=true | all-gather | bytes 491520 | tf_op jit(solution)/shard_map/all_gather | solution.py:100
  31.2 6.0 %collective-permute-start.7 = (bf16[1,40,16,1]{3,1,2,0:T(8,128)(2,1)S(1)}, bf16[1,40,16,1]{3,1,2,0:T(8,128)(2,1)S(1)}, u32[]{:S(2)}, u32[]{:S(2)}) collective-permute-start(bf16[1,40,16,1]{3,1,2,0:T(8,128)(2,1)S(1)} %get-tuple-element.114), channel_id=1, source_target_pairs={{2,0},{4,2},{6,4},{8,6},{10,8},{12,10},{14,12},{16,14},{18,16},{20... | collective-permute-start | bytes 3848 | tf_op jit(solution)/shard_map/ppermute | solution.py:21
  37.3 3.2 %collective-permute-start.6 = (bf16[1,40,1,128]{3,1,2,0:T(8,128)(2,1)S(1)}, bf16[1,40,1,128]{3,1,2,0:T(8,128)(2,1)S(1)}, u32[]{:S(2)}, u32[]{:S(2)}) collective-permute-start(bf16[1,40,1,128]{3,1,2,0:T(8,128)(2,1)S(1)} %get-tuple-element.112), channel_id=1, source_target_pairs={{32,0},{64,32},{96,64},{128,96},{160,128},{192,160},{224,192},{0,2... | collective-permute-start | bytes 30728 | tf_op jit(solution)/shard_map/ppermute | solution.py:21
  42.1 8.0 %gather_fusion.2 = bf16[2048,40]{1,0:T(8,128)(2,1)} fusion(bf16[40,2048]{0,1:T(8,128)(2,1)S(1)} %bitcast.258, s32[2048]{0:T(1024)S(1)} %fusion.77), kind=kCustom, calls=%fused_computation.2.clone | custom fusion | bytes 335872 | tf_op jit(solution)/shard_map/jit(_take)/gather | solution.py:121
  50.8 2.4 %all_gather.7 = bf16[80,2048]{1,0:T(8,128)(2,1)S(1)} all-gather(bf16[40,2048]{1,0:T(8,128)(2,1)S(1)} %bitcast.268), channel_id=1, replica_groups=mesh['lat_0'=2,'lat_1'=4,'lon_0'=2,'lon_1'=8,'lev'=2] {'lev'}, dimensions={0}, use_global_device_ids=true | all-gather | bytes 491520 | tf_op jit(solution)/shard_map/all_gather | solution.py:100
  53.8 8.0 %gather_fusion = bf16[2048,40]{1,0:T(8,128)(2,1)} fusion(bf16[40,2048]{0,1:T(8,128)(2,1)S(1)} %bitcast.257, s32[2048]{0:T(1024)S(1)} %fusion.77), kind=kCustom, calls=%fused_computation.clone | custom fusion | bytes 335872 | tf_op jit(solution)/shard_map/jit(_take)/gather | solution.py:121
  61.8 1.5 bitcast_convert_fusion.1
  63.8 4.7 %all_to_all.30 = bf16[2,16,40,128]{3,2,1,0:T(8,128)(2,1)} all-to-all(bf16[2,16,40,128]{3,2,1,0:T(8,128)(2,1)S(1)} %broadcast_in_dim.25), channel_id=1, replica_groups=mesh['lat_0'=2,'lat_1'=4,'lon_0'=2,'lon_1'=8,'lev'=2] {'lev'}, dimensions={0} | all-to-all | bytes 655360 | tf_op jit(solution)/shard_map/all_to_all | solution.py:40
  69.3 3.8 %all-to-all-start = ((bf16[2,16,40,128]{3,2,1,0:T(8,128)(2,1)}), bf16[2,16,40,128]{3,2,1,0:T(8,128)(2,1)S(1)}, u32[]{:S(2)}, u32[]{:S(2)}) async-start(bf16[2,16,40,128]{3,2,1,0:T(8,128)(2,1)} %broadcast_in_dim.21), calls=%async_computation | async-start | bytes 655360 | tf_op jit(solution)/shard_map/all_to_all | solution.py:40
  76.2 3.5 %all-to-all-start.2 = ((f32[2,40,80]{2,1,0:T(8,128)}), f32[2,40,80]{2,1,0:T(8,128)S(1)}, u32[]{:S(2)}, u32[]{:S(2)}) async-start(f32[2,40,80]{2,1,0:T(8,128)} %broadcast_in_dim.23), calls=%async_computation.2 | async-start | bytes 81920 | tf_op jit(solution)/shard_map/all_to_all | solution.py:40
  81.6 5.5 %gather_fusion.1 = f32[2048,40]{1,0:T(8,128)S(1)} fusion(f32[40,2048]{0,1:T(8,128)S(1)} %bitcast.256, s32[2048]{0:T(1024)S(1)} %fusion.78), kind=kCustom, calls=%fused_computation.1.clone | custom fusion | bytes 663552 | tf_op jit(solution)/shard_map/jit(_take)/gather | solution.py:131
  87.5 3.7 %all_to_all.31 = bf16[2,40,2048]{2,1,0:T(8,128)(2,1)S(1)} all-to-all(bf16[2,40,2048]{2,1,0:T(8,128)(2,1)S(1)} %broadcast_in_dim.24), channel_id=1, replica_groups=mesh['lat_0'=2,'lat_1'=4,'lon_0'=2,'lon_1'=8,'lev'=2] {'lev'}, dimensions={0} | all-to-all | bytes 655360 | tf_op jit(solution)/shard_map/all_to_all | solution.py:40
  91.9 1.3 copy.138
  93.2 7.6 %gather_fusion.3 = f32[2048,40]{1,0:T(8,128)} fusion(f32[40,2048]{0,1:T(8,128)S(1)} %bitcast.255, s32[2048]{0:T(1024)S(1)} %fusion.78), kind=kCustom, calls=%fused_computation.3.clone | custom fusion | bytes 663552 | tf_op jit(solution)/shard_map/jit(_take)/gather | solution.py:131
  102.0 6.0 %collective-permute-start.11 = (bf16[3,40,16,1]{3,1,2,0:T(8,128)(2,1)}, bf16[3,40,16,1]{3,1,2,0:T(8,128)(2,1)}, u32[]{:S(2)}, u32[]{:S(2)}) collective-permute-start(bf16[3,40,16,1]{3,1,2,0:T(8,128)(2,1)} %get-tuple-element.104), channel_id=1, source_target_pairs={{2,0},{4,2},{6,4},{8,6},{10,8},{12,10},{14,12},{16,14},{18,16},{20... | collective-permute-start | bytes 11528 | tf_op jit(solution)/shard_map/ppermute | solution.py:21
  107.9 3.2 %collective-permute-start.10 = (bf16[3,40,1,128]{3,1,2,0:T(8,128)(2,1)S(1)}, bf16[3,40,1,128]{3,1,2,0:T(8,128)(2,1)S(1)}, u32[]{:S(2)}, u32[]{:S(2)}) collective-permute-start(bf16[3,40,1,128]{3,1,2,0:T(8,128)(2,1)S(1)} %get-tuple-element.102), channel_id=1, source_target_pairs={{32,0},{64,32},{96,64},{128,96},{160,128},{192,160},{224,192},{0,2... | collective-permute-start | bytes 92168 | tf_op jit(solution)/shard_map/ppermute | solution.py:21
  111.8 6.7 %collective-permute-done.11 = bf16[3,40,16,1]{3,1,2,0:T(8,128)(2,1)} collective-permute-done((bf16[3,40,16,1]{3,1,2,0:T(8,128)(2,1)}, bf16[3,40,16,1]{3,1,2,0:T(8,128)(2,1)}, u32[]{:S(2)}, u32[]{:S(2)}) %collective-permute-start.11) | collective-permute-done | bytes 3872 | tf_op jit(solution)/shard_map/ppermute | solution.py:21
  118.5 5.5 %collective-permute-done.8 = bf16[3,40,16,1]{3,1,2,0:T(8,128)(2,1)} collective-permute-done((bf16[3,40,16,1]{3,1,2,0:T(8,128)(2,1)}, bf16[3,40,16,1]{3,1,2,0:T(8,128)(2,1)}, u32[]{:S(2)}, u32[]{:S(2)}) %collective-permute-start.8) | collective-permute-done | bytes 3872 | tf_op jit(solution)/shard_map/ppermute | solution.py:20
  124.0 2.9 %collective-permute-done.9 = bf16[3,40,1,128]{3,1,2,0:T(8,128)(2,1)S(1)} collective-permute-done((bf16[3,40,1,128]{3,1,2,0:T(8,128)(2,1)S(1)}, bf16[3,40,1,128]{3,1,2,0:T(8,128)(2,1)S(1)}, u32[]{:S(2)}, u32[]{:S(2)}) %collective-permute-start.9) | collective-permute-done | bytes 30752 | tf_op jit(solution)/shard_map/ppermute | solution.py:20
  127.0 1.9 %convert_multiply_fusion.1 = f32[3,40,18,130]{3,1,2,0:T(8,128)S(1)} fusion(bf16[3,40,16,1]{3,1,2,0:T(8,128)(2,1)} %collective-permute-done.11, bf16[3,40,16,1]{3,1,2,0:T(8,128)(2,1)} %collective-permute-done.8, bf16[3,40,1,128]{3,1,2,0:T(8,128)(2,1)S(1)} %collective-permute-done.10, bf16[1,40,16,128]{3,1,2,0:T(8,128)(2,1)S(1)} %get-tuple-element.109, ...), kind=kLoop, calls=%fused_computation.11 | loop fusion | flops 5335200 | bytes 1683912 | tf_op jit(solution)/shard_map/mul | solution.py:65
  129.6 4.1 %all_to_all.32 = bf16[2,40,2048]{2,1,0:T(8,128)(2,1)S(1)} all-to-all(bf16[2,40,2048]{2,1,0:T(8,128)(2,1)S(1)} %broadcast_in_dim.46), channel_id=1, replica_groups=mesh['lat_0'=2,'lat_1'=4,'lon_0'=2,'lon_1'=8,'lev'=2] {'lev'}, dimensions={0} | all-to-all | bytes 655360 | tf_op jit(solution)/shard_map/all_to_all | solution.py:40
  136.2 1.4 collective-permute-start.14
  140.3 12.0 %psum.35 = f32[]{:T(128)} all-reduce(f32[]{:T(128)S(6)} %add.190), channel_id=1, replica_groups=mesh['lat_0'=2,'lat_1'=4,'lon_0'=2,'lon_1'=8,'lev'=2] {'lat_0'}, use_global_device_ids=true, to_apply=%region_4.6 | all-reduce | flops 1 | bytes 8 | tf_op jit(solution)/shard_map/psum | solution.py:49
  152.3 7.0 %psum.36 = f32[]{:T(128)} all-reduce(f32[]{:T(128)} %psum.35), channel_id=1, replica_groups=mesh['lat_0'=2,'lat_1'=4,'lon_0'=2,'lon_1'=8,'lev'=2] {'lat_1'}, use_global_device_ids=true, to_apply=%region_5.7 | all-reduce | flops 1 | bytes 8 | tf_op jit(solution)/shard_map/psum | solution.py:49
  159.3 5.9 %psum.37 = f32[]{:T(128)} all-reduce(f32[]{:T(128)} %psum.36), channel_id=1, replica_groups=mesh['lat_0'=2,'lat_1'=4,'lon_0'=2,'lon_1'=8,'lev'=2] {'lon_0'}, use_global_device_ids=true, to_apply=%region_6.8 | all-reduce | flops 1 | bytes 8 | tf_op jit(solution)/shard_map/psum | solution.py:49
  165.2 11.6 %psum.38 = f32[]{:T(128)} all-reduce(f32[]{:T(128)} %psum.37), channel_id=1, replica_groups=mesh['lat_0'=2,'lat_1'=4,'lon_0'=2,'lon_1'=8,'lev'=2] {'lon_1'}, use_global_device_ids=true, to_apply=%region_7.9 | all-reduce | flops 1 | bytes 8 | tf_op jit(solution)/shard_map/psum | solution.py:49
  176.8 9.6 %psum.39 = f32[]{:T(128)} all-reduce(f32[]{:T(128)} %psum.38), channel_id=1, replica_groups=mesh['lat_0'=2,'lat_1'=4,'lon_0'=2,'lon_1'=8,'lev'=2] {'lev'}, use_global_device_ids=true, to_apply=%region_8.10 | all-reduce | flops 1 | bytes 8 | tf_op jit(solution)/shard_map/psum | solution.py:49
  (105 shorter events, 23.2 us)
Async XLA Ops:
  0.6 21.4 %copy-start.7 = (s32[1,1,2048]{2,1,0:T(1,128)S(1)}, s32[1,1,2048]{2,1,0:T(1,128)}, u32[]{:S(2)}) copy-start(s32[1,1,2048]{2,1,0:T(1,128)} %param.37) | copy-start | bytes 24580
  1.7 26.4 %copy-start = (f32[40,16,128]{2,1,0:T(8,128)S(1)}, f32[40,16,128]{2,1,0:T(8,128)}, u32[]{:S(2)}) copy-start(f32[40,16,128]{2,1,0:T(8,128)} %param.30) | copy-start | bytes 983044
  1.7 26.4 %copy-start.1 = (f32[40,16,128]{2,1,0:T(8,128)S(1)}, f32[40,16,128]{2,1,0:T(8,128)}, u32[]{:S(2)}) copy-start(f32[40,16,128]{2,1,0:T(8,128)} %param.29) | copy-start | bytes 983044
  1.8 26.4 %copy-start.2 = (f32[40,16,128]{2,1,0:T(8,128)S(1)}, f32[40,16,128]{2,1,0:T(8,128)}, u32[]{:S(2)}) copy-start(f32[40,16,128]{2,1,0:T(8,128)} %param.28) | copy-start | bytes 983044
  1.8 26.4 %copy-start.8 = (f32[40]{0:T(128)S(1)}, f32[40]{0:T(128)}, u32[]{:S(2)}) copy-start(f32[40]{0:T(128)} %param.31) | copy-start | bytes 484
  1.9 25.9 %collective-permute-start.3 = (bf16[1,40,16,1]{3,1,2,0:T(8,128)(2,1)S(1)}, bf16[1,40,16,1]{3,1,2,0:T(8,128)(2,1)S(1)}, u32[]{:S(2)}, u32[]{:S(2)}) collective-permute-start(bf16[1,40,16,1]{3,1,2,0:T(8,128)(2,1)S(1)} %get-tuple-element.118), channel_id=1, source_target_pairs={{2,0},{4,2},{6,4},{8,6},{10,8},{12,10},{14,12},{16,14},{18,16},{20... | collective-permute-start | bytes 3848 | tf_op jit(solution)/shard_map/ppermute | solution.py:21
  10.8 17.0 %collective-permute-start = (bf16[1,40,16,1]{3,1,2,0:T(8,128)(2,1)S(1)}, bf16[1,40,16,1]{3,1,2,0:T(8,128)(2,1)S(1)}, u32[]{:S(2)}, u32[]{:S(2)}) collective-permute-start(bf16[1,40,16,1]{3,1,2,0:T(8,128)(2,1)S(1)} %get-tuple-element.117), channel_id=1, source_target_pairs={{0,2},{2,4},{4,6},{6,8},{8,10},{10,12},{12,14},{14,16},{16,18},{18... | collective-permute-start | bytes 3848 | tf_op jit(solution)/shard_map/ppermute | solution.py:20
  10.8 17.0 %collective-permute-start.2 = (bf16[1,40,1,128]{3,1,2,0:T(8,128)(2,1)S(1)}, bf16[1,40,1,128]{3,1,2,0:T(8,128)(2,1)S(1)}, u32[]{:S(2)}, u32[]{:S(2)}) collective-permute-start(bf16[1,40,1,128]{3,1,2,0:T(8,128)(2,1)S(1)} %get-tuple-element.116), channel_id=1, source_target_pairs={{32,0},{64,32},{96,64},{128,96},{160,128},{192,160},{224,192},{0,2... | collective-permute-start | bytes 30728 | tf_op jit(solution)/shard_map/ppermute | solution.py:21
  13.6 14.3 %collective-permute-start.1 = (bf16[1,40,1,128]{3,1,2,0:T(8,128)(2,1)S(1)}, bf16[1,40,1,128]{3,1,2,0:T(8,128)(2,1)S(1)}, u32[]{:S(2)}, u32[]{:S(2)}) collective-permute-start(bf16[1,40,1,128]{3,1,2,0:T(8,128)(2,1)S(1)} %get-tuple-element.115), channel_id=1, source_target_pairs={{0,32},{32,64},{64,96},{96,128},{128,160},{160,192},{192,224},{224... | collective-permute-start | bytes 30728 | tf_op jit(solution)/shard_map/ppermute | solution.py:20
  14.9 48.8 %all-to-all-start.1 = ((bf16[2,128,40]{1,2,0:T(8,128)(2,1)}), bf16[2,128,40]{1,2,0:T(8,128)(2,1)S(1)}, u32[]{:S(2)}, u32[]{:S(2)}) async-start(bf16[2,128,40]{1,2,0:T(8,128)(2,1)} %broadcast_in_dim.22), calls=%async_computation.1 | async-start | bytes 40960 | tf_op jit(solution)/shard_map/all_to_all | solution.py:40
  27.8 2.9 %copy-start.5 = (f32[40,80]{1,0:T(8,128)S(1)}, f32[40,80]{1,0:T(8,128)}, u32[]{:S(2)}) copy-start(f32[40,80]{1,0:T(8,128)} %param.32) | copy-start | bytes 38404
  31.2 18.8 %collective-permute-start.7 = (bf16[1,40,16,1]{3,1,2,0:T(8,128)(2,1)S(1)}, bf16[1,40,16,1]{3,1,2,0:T(8,128)(2,1)S(1)}, u32[]{:S(2)}, u32[]{:S(2)}) collective-permute-start(bf16[1,40,16,1]{3,1,2,0:T(8,128)(2,1)S(1)} %get-tuple-element.114), channel_id=1, source_target_pairs={{2,0},{4,2},{6,4},{8,6},{10,8},{12,10},{14,12},{16,14},{18,16},{20... | collective-permute-start | bytes 3848 | tf_op jit(solution)/shard_map/ppermute | solution.py:21
  37.3 12.8 %collective-permute-start.4 = (bf16[1,40,16,1]{3,1,2,0:T(8,128)(2,1)S(1)}, bf16[1,40,16,1]{3,1,2,0:T(8,128)(2,1)S(1)}, u32[]{:S(2)}, u32[]{:S(2)}) collective-permute-start(bf16[1,40,16,1]{3,1,2,0:T(8,128)(2,1)S(1)} %get-tuple-element.113), channel_id=1, source_target_pairs={{0,2},{2,4},{4,6},{6,8},{8,10},{10,12},{12,14},{14,16},{16,18},{18... | collective-permute-start | bytes 3848 | tf_op jit(solution)/shard_map/ppermute | solution.py:20
  37.3 12.8 %collective-permute-start.6 = (bf16[1,40,1,128]{3,1,2,0:T(8,128)(2,1)S(1)}, bf16[1,40,1,128]{3,1,2,0:T(8,128)(2,1)S(1)}, u32[]{:S(2)}, u32[]{:S(2)}) collective-permute-start(bf16[1,40,1,128]{3,1,2,0:T(8,128)(2,1)S(1)} %get-tuple-element.112), channel_id=1, source_target_pairs={{32,0},{64,32},{96,64},{128,96},{160,128},{192,160},{224,192},{0,2... | collective-permute-start | bytes 30728 | tf_op jit(solution)/shard_map/ppermute | solution.py:21
  40.5 9.6 %collective-permute-start.5 = (bf16[1,40,1,128]{3,1,2,0:T(8,128)(2,1)S(1)}, bf16[1,40,1,128]{3,1,2,0:T(8,128)(2,1)S(1)}, u32[]{:S(2)}, u32[]{:S(2)}) collective-permute-start(bf16[1,40,1,128]{3,1,2,0:T(8,128)(2,1)S(1)} %get-tuple-element.111), channel_id=1, source_target_pairs={{0,32},{32,64},{64,96},{96,128},{128,160},{160,192},{192,224},{224... | collective-permute-start | bytes 30728 | tf_op jit(solution)/shard_map/ppermute | solution.py:20
  63.3 9.8 %copy-start.3 = (bf16[1,1,1,16,128,128]{4,5,3,2,1,0:T(8,128)(2,1)S(1)}, bf16[1,1,1,16,128,128]{4,5,3,2,1,0:T(8,128)(2,1)}, u32[]{:S(2)}) copy-start(bf16[1,1,1,16,128,128]{4,5,3,2,1,0:T(8,128)(2,1)} %copy.147) | copy-start | bytes 1572868
  63.7 10.7 %copy-start.6 = (bf16[128,40]{0,1:T(8,128)(2,1)S(1)}, bf16[128,40]{0,1:T(8,128)(2,1)}, u32[]{:S(2)}) copy-start(bf16[128,40]{0,1:T(8,128)(2,1)} %param.33) | copy-start | bytes 30724
  63.7 10.7 %copy-start.9 = (f32[128]{0:T(128)S(1)}, f32[128]{0:T(128)}, u32[]{:S(2)}) copy-start(f32[128]{0:T(128)} %param.34) | copy-start | bytes 1540
  69.3 6.3 %all-to-all-start = ((bf16[2,16,40,128]{3,2,1,0:T(8,128)(2,1)}), bf16[2,16,40,128]{3,2,1,0:T(8,128)(2,1)S(1)}, u32[]{:S(2)}, u32[]{:S(2)}) async-start(bf16[2,16,40,128]{3,2,1,0:T(8,128)(2,1)} %broadcast_in_dim.21), calls=%async_computation | async-start | bytes 655360 | tf_op jit(solution)/shard_map/all_to_all | solution.py:40
  76.2 11.2 %all-to-all-start.2 = ((f32[2,40,80]{2,1,0:T(8,128)}), f32[2,40,80]{2,1,0:T(8,128)S(1)}, u32[]{:S(2)}, u32[]{:S(2)}) async-start(f32[2,40,80]{2,1,0:T(8,128)} %broadcast_in_dim.23), calls=%async_computation.2 | async-start | bytes 81920 | tf_op jit(solution)/shard_map/all_to_all | solution.py:40
  100.8 10.4 %copy-start.4 = (f32[2048,40]{1,0:T(8,128)S(1)}, f32[2048,40]{1,0:T(8,128)}, u32[]{:S(2)}) copy-start(f32[2048,40]{1,0:T(8,128)} %gather_fusion.3) | copy-start | bytes 983044
  102.0 16.5 %collective-permute-start.11 = (bf16[3,40,16,1]{3,1,2,0:T(8,128)(2,1)}, bf16[3,40,16,1]{3,1,2,0:T(8,128)(2,1)}, u32[]{:S(2)}, u32[]{:S(2)}) collective-permute-start(bf16[3,40,16,1]{3,1,2,0:T(8,128)(2,1)} %get-tuple-element.104), channel_id=1, source_target_pairs={{2,0},{4,2},{6,4},{8,6},{10,8},{12,10},{14,12},{16,14},{18,16},{20... | collective-permute-start | bytes 11528 | tf_op jit(solution)/shard_map/ppermute | solution.py:21
  107.9 16.1 %collective-permute-start.8 = (bf16[3,40,16,1]{3,1,2,0:T(8,128)(2,1)}, bf16[3,40,16,1]{3,1,2,0:T(8,128)(2,1)}, u32[]{:S(2)}, u32[]{:S(2)}) collective-permute-start(bf16[3,40,16,1]{3,1,2,0:T(8,128)(2,1)} %get-tuple-element.103), channel_id=1, source_target_pairs={{0,2},{2,4},{4,6},{6,8},{8,10},{10,12},{12,14},{14,16},{16,18},{18... | collective-permute-start | bytes 11528 | tf_op jit(solution)/shard_map/ppermute | solution.py:20
  107.9 16.1 %collective-permute-start.10 = (bf16[3,40,1,128]{3,1,2,0:T(8,128)(2,1)S(1)}, bf16[3,40,1,128]{3,1,2,0:T(8,128)(2,1)S(1)}, u32[]{:S(2)}, u32[]{:S(2)}) collective-permute-start(bf16[3,40,1,128]{3,1,2,0:T(8,128)(2,1)S(1)} %get-tuple-element.102), channel_id=1, source_target_pairs={{32,0},{64,32},{96,64},{128,96},{160,128},{192,160},{224,192},{0,2... | collective-permute-start | bytes 92168 | tf_op jit(solution)/shard_map/ppermute | solution.py:21
  111.2 15.8 %collective-permute-start.9 = (bf16[3,40,1,128]{3,1,2,0:T(8,128)(2,1)S(1)}, bf16[3,40,1,128]{3,1,2,0:T(8,128)(2,1)S(1)}, u32[]{:S(2)}, u32[]{:S(2)}) collective-permute-start(bf16[3,40,1,128]{3,1,2,0:T(8,128)(2,1)S(1)} %get-tuple-element.101), channel_id=1, source_target_pairs={{0,32},{32,64},{64,96},{96,128},{128,160},{160,192},{192,224},{224... | collective-permute-start | bytes 92168 | tf_op jit(solution)/shard_map/ppermute | solution.py:20
  134.7 52.3 %collective-permute-start.15 = (bf16[3,40,16,1]{3,1,2,0:T(8,128)(2,1)S(1)}, bf16[3,40,16,1]{3,1,2,0:T(8,128)(2,1)S(1)}, u32[]{:S(2)}, u32[]{:S(2)}) collective-permute-start(bf16[3,40,16,1]{3,1,2,0:T(8,128)(2,1)S(1)} %get-tuple-element.100), channel_id=1, source_target_pairs={{2,0},{4,2},{6,4},{8,6},{10,8},{12,10},{14,12},{16,14},{18,16},{20... | collective-permute-start | bytes 11528 | tf_op jit(solution)/shard_map/ppermute | solution.py:21
  135.3 51.7 %collective-permute-start.12 = (bf16[3,40,16,1]{3,1,2,0:T(8,128)(2,1)S(1)}, bf16[3,40,16,1]{3,1,2,0:T(8,128)(2,1)S(1)}, u32[]{:S(2)}, u32[]{:S(2)}) collective-permute-start(bf16[3,40,16,1]{3,1,2,0:T(8,128)(2,1)S(1)} %get-tuple-element.99), channel_id=1, source_target_pairs={{0,2},{2,4},{4,6},{6,8},{8,10},{10,12},{12,14},{14,16},{16,18},{18... | collective-permute-start | bytes 11528 | tf_op jit(solution)/shard_map/ppermute | solution.py:20
  136.2 50.8 %collective-permute-start.14 = (bf16[3,40,1,128]{3,1,2,0:T(8,128)(2,1)S(1)}, bf16[3,40,1,128]{3,1,2,0:T(8,128)(2,1)S(1)}, u32[]{:S(2)}, u32[]{:S(2)}) collective-permute-start(bf16[3,40,1,128]{3,1,2,0:T(8,128)(2,1)S(1)} %get-tuple-element.98), channel_id=1, source_target_pairs={{32,0},{64,32},{96,64},{128,96},{160,128},{192,160},{224,192},{0,2... | collective-permute-start | bytes 92168 | tf_op jit(solution)/shard_map/ppermute | solution.py:21
  137.6 49.4 %collective-permute-start.13 = (bf16[3,40,1,128]{3,1,2,0:T(8,128)(2,1)S(1)}, bf16[3,40,1,128]{3,1,2,0:T(8,128)(2,1)S(1)}, u32[]{:S(2)}, u32[]{:S(2)}) collective-permute-start(bf16[3,40,1,128]{3,1,2,0:T(8,128)(2,1)S(1)} %get-tuple-element.97), channel_id=1, source_target_pairs={{0,32},{32,64},{64,96},{96,128},{128,160},{160,192},{192,224},{224... | collective-permute-start | bytes 92168 | tf_op jit(solution)/shard_map/ppermute | solution.py:20
where the time goes:
time: 191 us; the launch traced here: 190 us
  blocking collectives  63 us (33%)
  starting transfers between devices  44.9 us (24%)
  local copies, waits for them, and re-layouts  41.2 us (22%)
  waiting for transfers between devices  15.2 us (8%)
  other arithmetic  14.9 us (8%)
  between operations  5.55 us (3%)
  matrix products  5.44 us (3%)
    psum x5, blocking collectives, over_axes(): shard = lax.psum(shard, axis)  46.1 us
    ppermute x8, starting transfers between devices, with_halo(): lax.ppermute(leading, axis, [(b, a) for a, b in up])  32.3 us
    gather x2, local copies, waits for them, and re-layouts, take_profiles(): selected_columns = jnp.take(state.reshape(level_count, -1), columns, axis=1)  16 us
    gather x3, local copies, waits for them, and re-layouts, place_back(): return jnp.take(dispersed_blocks, inverse, axis=1).reshape(shape)  13.4 us
    all_to_all x3, blocking collectives, from_everyone(): return lax.all_to_all(copies, axis, split_axis=0, concat_axis=0, tiled=True)  12.5 us
    all_to_all x3, starting transfers between devices, from_everyone(): return lax.all_to_all(copies, axis, split_axis=0, concat_axis=0, tiled=True)  11.7 us
    ppermute x8, waiting for transfers between devices, with_halo(): lax.ppermute(last, axis, up)  8.48 us
    ppermute x8, waiting for transfers between devices, with_halo(): lax.ppermute(leading, axis, [(b, a) for a, b in up])  6.68 us
  transfers between devices with their start and end apart: 19, of which 3 were waited for; matrix products, arithmetic and copies ran while one was open for 22% of the time, Pallas kernels for 0%

commit v1 on v0

v1 whole, which is shorter than its diff:
```python
import functools

import jax
import jax.numpy as jnp
from jax import lax
from jax.experimental import pallas as pl
from jax.experimental.pallas import tpu as pltpu
from jax.sharding import PartitionSpec as P

F32 = jnp.float32
BF16 = jnp.bfloat16
MESH = pl.DeviceIdType.MESH
HALO = 4
GROUPS = (0, 3, 6, 8, 10, 13)
LANES = 128


def dot(a, b):
    return lax.dot_general(a, b, (((1,), (0,)), ((), ())), preferred_element_type=F32)


def dot_nt(a, b):
    return lax.dot_general(a, b, (((1,), (1,)), ((), ())), preferred_element_type=F32)


def dot_tn(a, b):
    return lax.dot_general(a, b, (((0,), (0,)), ((), ())), preferred_element_type=F32)


def iota(shape, dim):
    return lax.broadcasted_iota(jnp.int32, shape, dim)


def one_hot(condition):
    return jnp.where(condition, 1.0, 0.0).astype(BF16)


def at_row(e):
    return slice(LANES * e, LANES * (e + 1))


def kernel(
    sizes,
    inc_h, u_h, v_h, dif_h, mix_h, jac_h, w_h, y_h, cnt_s, lut_h,
    out_ref, cost_ref,
    inc, u, v, dif, mix, jac, w, y, lut,
    own, partner, misc, misc_in, full,
    south, north, south_in, north_in,
    strip_e, strip_w, strip_in, strip_s, strip_n,
    slots, pick, grid, grid_s, grid_n, edge, edge_in, edge_s, edge_n,
    x0, x1, hu, hv, sm, f1, back, back_in,
    load_sem, send_sem, recv_sem,
):
    nlat, nlon, half, rows = sizes
    full_levels = 2 * half
    i, j, h = lax.axis_index("lat"), lax.axis_index("lon"), lax.axis_index("lev")
    other = 1 - h
    up, down = lax.rem(i + 1, nlat), lax.rem(i + nlat - 1, nlat)
    east, west = lax.rem(j + 1, nlon), lax.rem(j + nlon - 1, nlon)
    side = lax.rem(j + nlon - 1 + 2 * h, nlon)

    barrier = pltpu.get_barrier_semaphore()
    senders = [(up, j, h), (down, j, h), (i, j, other)]
    senders += [(a, side, k) for a in (i, up, down) for k in (0, 1)]
    for device in senders:
        pl.semaphore_signal(barrier, inc=1, device_id=device, device_id_type=MESH)

    loads = {}
    pairs = ((inc_h, inc), (u_h, u), (v_h, v), (dif_h, dif), (mix_h, mix), (jac_h, jac), (w_h, w), (lut_h, lut), (y_h, y))
    for n, (source, target) in enumerate(pairs):
        loads[n] = pltpu.make_async_copy(source, target, load_sem.at[n])
        loads[n].start()

    def remote(n, source, target, device, arrival=None):
        return pltpu.make_async_remote_copy(
            src_ref=source,
            dst_ref=target,
            send_sem=send_sem.at[n],
            recv_sem=recv_sem.at[n if arrival is None else arrival],
            device_id=device,
            device_id_type=MESH,
        )

    for n in range(3):
        loads[n].wait()
    fields = (inc, u, v)

    def own_row(f, r):
        value = fields[f][pl.ds(r, half, stride=rows), :]
        return value if f == 0 else 0.5 * value

    for q in range(rows // 2):
        for f in range(3):
            own[f, q] = jnp.concatenate([own_row(f, 2 * q), own_row(f, 2 * q + 1)], axis=0).astype(BF16)

    wide = (32, 3 * LANES)
    number, lane = iota(wide, 0), iota(wide, 1)
    inner = number & 15
    west_edge = number >> 4
    spot = (inner >> 2) * LANES + (inner & 3) + (1 - west_edge) * (LANES - HALO)
    selector = one_hot((spot == lane) & (inner < 12))
    for g, start in enumerate(GROUPS):
        block = jnp.concatenate(
            [
                jnp.concatenate([own_row(f, start + t) for t in range(3)], axis=0).astype(BF16)
                for f in range(3)
            ],
            axis=1,
        )
        strip = dot_nt(selector, block).astype(BF16)
        strip_e[g, :, 0 : 3 * half] = strip[0:16]
        strip_w[g, :, 0 : 3 * half] = strip[16:32]
        strip_e[g, :, 3 * half : LANES] = jnp.zeros((16, LANES - 3 * half), BF16)
        strip_w[g, :, 3 * half : LANES] = jnp.zeros((16, LANES - 3 * half), BF16)

    for n in range(3, 8):
        loads[n].wait()
    misc[0] = jnp.zeros((half, LANES), F32)
    misc[0, :, 0:full_levels] = mix[...]
    eye = iota((half, half), 0) == iota((half, half), 1)
    misc[1] = dot_nt(one_hot(eye), jac[...])
    column = jnp.sum(jnp.where(eye, dif[...], 0.0), axis=1, keepdims=True)
    misc[2] = jnp.broadcast_to(column, (half, LANES))

    pl.semaphore_wait(barrier, len(senders))

    copies = [
        remote(2, own.at[:, 6:8], south, (up, j, h)),
        remote(3, own.at[:, 0:2], north, (down, j, h)),
        remote(6, strip_e, strip_in.at[h], (i, east, 0), 6 + h),
        remote(7, strip_w, strip_in.at[h], (i, west, 1), 6 + h),
        remote(8, strip_e.at[5], strip_s.at[h], (up, east, 0), 8 + h),
        remote(9, strip_e.at[0], strip_n.at[h], (down, east, 0), 10 + h),
        remote(10, strip_w.at[5], strip_s.at[h], (up, west, 1), 8 + h),
        remote(11, strip_w.at[0], strip_n.at[h], (down, west, 1), 10 + h),
        remote(1, misc, misc_in, (i, j, other)),
        remote(0, own, partner, (i, j, other)),
    ]
    for copy in copies:
        copy.start()

    table = lut[...]
    low = dot_nt(one_hot(iota((LANES, LANES), 0) == iota((LANES, LANES), 1)), (table & 255).astype(F32).astype(BF16))
    pair_lane = iota((LANES, 2 * LANES), 1).astype(F32)
    for s in range(16):
        pick[LANES * s : LANES * (s + 1)] = one_hot(jnp.broadcast_to(low[:, s : s + 1], (LANES, 2 * LANES)) == pair_lane)
    pair_of = (table >> 8).astype(F32)

    count = cnt_s[0, 0]
    live = [jnp.where(count > s, 1.0, 0.0).astype(F32) for s in range(16)]
    loads[8].wait()
    w_row = w[...]
    w_column = jnp.sum(
        jnp.where(iota((LANES, LANES), 0) == iota((LANES, LANES), 1), w_row, 0.0), axis=1, keepdims=True
    )
    squares = jnp.zeros((LANES, LANES), F32)
    for s in range(16):
        first, second = y[s].astype(F32), y[16 + s].astype(F32)
        squares = squares + live[s] * (first * first + second * second)
    squares = squares * w_column

    copies[8].wait_recv()
    here, there = pl.ds(pl.multiple_of(h * half, 8), half), pl.ds(pl.multiple_of(other * half, 8), half)
    for n in range(3):
        full[n, here, :] = misc[n]
        full[n, there, :] = misc_in[n]
    mixing = full[0][:, 0:full_levels].astype(BF16)
    eye80 = one_hot(iota((full_levels, full_levels), 0) == iota((full_levels, full_levels), 1))
    mixing_back = dot_nt(eye80, full[0].astype(BF16)[:, 0:full_levels]) if False else dot_tn(mixing, eye80)
    mixing_back = mixing_back.astype(BF16)
    jac_t = full[1].astype(BF16)
    weighted = (full[1] * w_row).astype(BF16)
    gram = dot_nt(weighted, jac_t).astype(BF16)

    for s in range(16):
        span = slice(LANES * s, LANES * (s + 1))
        first = dot(weighted, y[s]) * live[s]
        second = dot(weighted, y[16 + s]) * live[s]
        slots[:, span] = jnp.concatenate(
            [first, second, jnp.broadcast_to(live[s], (16, LANES))], axis=0
        ).astype(BF16)
    for q in range(rows // 2):
        masked = jnp.concatenate(
            [
                slots[:, LANES * s : LANES * (s + 1)]
                * jnp.broadcast_to(jnp.where(pair_of[s : s + 1, :] == q, 1.0, 0.0), (slots.shape[0], LANES)).astype(BF16)
                for s in range(16)
            ],
            axis=1,
        )
        grid[:, 2 * LANES * q : 2 * LANES * (q + 1)] = dot(masked, pick[...]).astype(BF16)

    def edge_selector(core):
        number, lane = iota((16, 4 * LANES), 0), iota((16, 4 * LANES), 1)
        return one_hot((number >> 2) * LANES + (number & 3) + core * (LANES - HALO) == lane)

    outgoing, incoming = edge_selector(h), edge_selector(other)
    depth = slots.shape[0]
    for q in range(4):
        block = jnp.concatenate([grid[:, at_row(4 * g + q)] for g in range(4)], axis=1)
        edge[:, 256 * q : 256 * q + depth] = dot_nt(outgoing, block).astype(BF16)
        edge[:, 256 * q + depth : 256 * (q + 1)] = jnp.zeros((16, 256 - depth), BF16)
    late = [
        remote(12, grid.at[:, 14 * LANES : 16 * LANES], grid_s, (up, j, h)),
        remote(13, grid.at[:, 0 : 2 * LANES], grid_n, (down, j, h)),
        remote(14, edge, edge_in, (i, side, other)),
        remote(15, edge.at[:, 768:1024], edge_s, (up, side, other)),
        remote(16, edge.at[:, 0:256], edge_n, (down, side, other)),
    ]
    for copy in late:
        copy.start()

    copies[0].wait_recv()
    relay_s = remote(4, south, south_in, (i, j, other))
    relay_s.start()
    copies[1].wait_recv()
    relay_n = remote(5, north, north_in, (i, j, other))
    relay_n.start()

    lane_row = iota((1, LANES), 1)
    patched = jnp.where(h == 0, lane_row - (LANES - HALO), HALO - 1 - lane_row) >= 0
    own_lanes = jnp.where(h == 0, LANES // 2 - 1 - lane_row, lane_row - LANES // 2) >= 0
    number, lane = iota((16, 3 * LANES), 0), iota((16, 3 * LANES), 1)
    place = one_hot(((number >> 2) * LANES + (number & 3) + other * (LANES - HALO) == lane) & (number < 12))
    mask_s = jnp.where(i > 0, 1.0, 0.0).astype(F32)
    mask_n = jnp.where(i < nlat - 1, 1.0, 0.0).astype(F32)

    def row_mask(e):
        return mask_s if e < HALO else mask_n if e >= HALO + rows else None

    def keep(e, value):
        mask = row_mask(e)
        return value if mask is None else value * mask

    targets = (x0, hu, hv)

    def assemble(e, sources, patches):
        for f in range(3):
            for span, source, patch in zip((here, there), sources, patches):
                value = source[f]
                if patch is not None:
                    value = jnp.where(patched, patch[:, at_row(f)], value)
                targets[f][span, at_row(e)] = keep(e, value)

    def rows_of(ref, q):
        blocks = [ref[f, q].astype(F32) for f in range(3)]
        return [[block[half * t : half * (t + 1)] for block in blocks] for t in (0, 1)]

    def patch_of(ref):
        return dot_tn(ref[:, 0 : 3 * half], place)

    copies[9].wait_recv()
    for k in (0, 1):
        remote(6, strip_e, strip_in.at[k], (i, east, 0), 6 + k).wait_recv()
    group_of = {}
    for r in range(rows):
        g = max(n for n, start in enumerate(GROUPS) if start <= r and r < start + 3)
        if r in (6, 7, 8):
            g = 2
        if r in (9, 10):
            g = 3
        group_of[r] = (g, r - GROUPS[g])
    found = {}

    def patches_for(r):
        g, t = group_of[r]
        if g not in found:
            found.clear()
            found[g] = (patch_of(strip_in.at[h, g]), patch_of(strip_in.at[other, g]))
        return [value[half * t : half * (t + 1)] for value in found[g]]

    for q in range(rows // 2):
        mine, theirs = rows_of(own, q), rows_of(partner, q)
        for t in (0, 1):
            r = 2 * q + t
            assemble(HALO + r, (mine[t], theirs[t]), patches_for(r))
    relay_s.wait_recv()
    relay_n.wait_recv()
    for k in (0, 1):
        remote(8, strip_e.at[5], strip_s.at[k], (i, east, 0), 8 + k).wait_recv()
        remote(9, strip_e.at[0], strip_n.at[k], (i, east, 0), 10 + k).wait_recv()
    patch = (patch_of(strip_s.at[h]), patch_of(strip_s.at[other]))
    for q in (0, 1):
        mine, theirs = rows_of(south, q), rows_of(south_in, q)
        for t in (0, 1):
            e = 2 * q + t
            fit = [None if e == 0 else value[half * (e - 1) : half * e] for value in patch]
            assemble(e, (mine[t], theirs[t]), fit)
    patch = (patch_of(strip_n.at[h]), patch_of(strip_n.at[other]))
    for q in (0, 1):
        mine, theirs = rows_of(north, q), rows_of(north_in, q)
        for t in (0, 1):
            e = 2 * q + t
            fit = [None if e == 3 else value[half * e : half * (e + 1)] for value in patch]
            assemble(HALO + rows + e, (mine[t], theirs[t]), fit)

    diffusion = full[2]
    centre = 1.0 - 4.0 * diffusion

    def step_row(x, e):
        value, above, below = x[:, at_row(e)], x[:, at_row(e + 1)], x[:, at_row(e - 1)]
        eastern = pltpu.roll(value, LANES - 1, 1)
        western = pltpu.roll(value, 1, 1)
        return (
            centre * value
            + diffusion * ((above + below) + (eastern + western))
            + hu[:, at_row(e)] * (western - eastern)
            + hv[:, at_row(e)] * (below - above)
        )

    def back_row(x, e):
        value, above, below = x[:, at_row(e)], x[:, at_row(e + 1)], x[:, at_row(e - 1)]
        spread, drift = diffusion * value, hu[:, at_row(e)] * value
        eastern = pltpu.roll(spread + drift, LANES - 1, 1)
        western = pltpu.roll(spread - drift, 1, 1)
        return (
            centre * value
            + (eastern + western)
            + (diffusion + hv[:, at_row(e + 1)]) * above
            + (diffusion - hv[:, at_row(e - 1)]) * below
        )

    def coupled(matrix, values):
        joined = jnp.concatenate(values, axis=1).astype(BF16)
        mixed = dot(matrix, joined)
        return [value + mixed[:, at_row(n)] for n, value in enumerate(values)]

    def pairwise(first, last):
        return [tuple(range(e, min(e + 2, last + 1))) for e in range(first, last + 1, 2)]

    for copy in late:
        copy.wait_recv()
    for q in range(4):
        value = dot_tn(edge_in[:, 256 * q : 256 * q + depth], incoming)
        for g in range(4):
            r = 4 * g + q
            f1[:, at_row(r + 2)] = jnp.where(patched, value[:, at_row(g)], grid[:, at_row(r)].astype(F32))
    f1[:, at_row(0)] = grid_s[:, at_row(0)].astype(F32)
    value = dot_tn(edge_s[:, 0:depth], incoming)
    f1[:, at_row(1)] = jnp.where(patched, value[:, at_row(3)], grid_s[:, at_row(1)].astype(F32))
    value = dot_tn(edge_n[:, 0:depth], incoming)
    f1[:, at_row(18)] = jnp.where(patched, value[:, at_row(0)], grid_n[:, at_row(0)].astype(F32))
    f1[:, at_row(19)] = grid_n[:, at_row(1)].astype(F32)

    for pair in pairwise(1, 22):
        values = coupled(mixing, [step_row(x0, e) for e in pair])
        for e, value in zip(pair, values):
            x1[:, at_row(e)] = keep(e, value)

    total = jnp.zeros((full_levels, LANES), F32)

    def forced(states, pair, step, total):
        halves = [state.astype(BF16) for state in states]
        image = dot(gram, jnp.concatenate(halves, axis=1))
        result = []
        for n, e in enumerate(pair):
            moved = f1[full_levels * step : full_levels * (step + 1), at_row(e - 2)]
            alive = f1[2 * full_levels : 2 * full_levels + 1, at_row(e - 2)]
            force = alive * image[:, at_row(n)] - moved
            if HALO <= e < HALO + rows:
                total = total + halves[n].astype(F32) * (force - moved)
            result.append(force)
        return result, total

    for pair in pairwise(2, 21):
        states = coupled(mixing, [step_row(x1, e) for e in pair])
        forces, total = forced(states, pair, 1, total)
        for e, value in zip(pair, coupled(mixing_back, forces)):
            x0[:, at_row(e)] = keep(e, value)

    for pair in pairwise(3, 20):
        forces, total = forced([x1[:, at_row(e)] for e in pair], pair, 0, total)
        values = [back_row(x0, e) + force for e, force in zip(pair, forces)]
        for e, value in zip(pair, coupled(mixing_back, values)):
            sm[:, at_row(e)] = keep(e, value)

    for r in range(rows):
        x1[:, at_row(r)] = back_row(sm, r + HALO)
    for q in range(rows // 2):
        back[q] = jnp.concatenate([x1[there, at_row(2 * q)], x1[there, at_row(2 * q + 1)]], axis=0).astype(BF16)
    final = remote(17, back, back_in, (i, j, other))
    final.start()

    increment = inc[...]
    part = 0.5 * jnp.sum(increment * increment, axis=0, keepdims=True)
    part = part + 0.25 * jnp.sum(squares, axis=0, keepdims=True)
    part = part + 0.5 * jnp.sum(jnp.where(own_lanes, total, 0.0), axis=0, keepdims=True)
    cost_ref[...] = part

    final.wait_recv()
    for q in range(rows // 2):
        received = back_in[q].astype(F32)
        for t in (0, 1):
            r = 2 * q + t
            adjoint = jnp.where(own_lanes, x1[here, at_row(r)], received[half * t : half * (t + 1)])
            out_ref[pl.ds(r, half, stride=rows), :] = inc[pl.ds(r, half, stride=rows), :] + adjoint
    for copy in copies + late + [relay_s, relay_n, final]:
        copy.wait_send()


def body(nlat, nlon, increment, wind_u, wind_v, diffusion, mixing, jacobian, obs_weight, innovation, counts, column_lookup):
    half, rows, width = increment.shape
    channels = jacobian.shape[0]
    wide = (HALO * 2 + rows) * width
    levels = 2 * half
    depth = 2 * levels + 16
    anywhere = pl.BlockSpec(memory_space=pl.ANY)
    vmem = pl.BlockSpec(memory_space=pltpu.VMEM)
    smem = pl.BlockSpec(memory_space=pltpu.SMEM)
    grid_size = rows * width
    strip = (16, width)
    scratch = [
        ((half * rows, width), F32), ((half * rows, width), F32), ((half * rows, width), F32),
        ((1, half), F32), ((half, levels), F32), ((channels, half), BF16), ((1, channels), F32),
        ((32, channels, width), BF16), ((16, width), jnp.int32),
        ((3, 8, levels, width), BF16), ((3, 8, levels, width), BF16),
        ((3, half, width), F32), ((3, half, width), F32), ((3, levels, width), F32),
        ((3, 2, levels, width), BF16), ((3, 2, levels, width), BF16),
        ((3, 2, levels, width), BF16), ((3, 2, levels, width), BF16),
        ((6, *strip), BF16), ((6, *strip), BF16), ((2, 6, *strip), BF16), ((2, *strip), BF16), ((2, *strip), BF16),
        ((depth, grid_size), BF16), ((grid_size, 2 * width), BF16), ((depth, grid_size), BF16),
        ((depth, 2 * width), BF16), ((depth, 2 * width), BF16),
        ((16, 1024), BF16), ((16, 1024), BF16), ((16, 256), BF16), ((16, 256), BF16),
        ((levels, wide), F32), ((levels, wide), F32), ((levels, wide), F32), ((levels, wide), F32), ((levels, wide), F32),
        ((depth, 20 * width), F32),
        ((8, levels, width), BF16), ((8, levels, width), BF16),
    ]
    gradient, part = pl.pallas_call(
        functools.partial(kernel, (nlat, nlon, half, rows)),
        out_shape=(
            jax.ShapeDtypeStruct((half * rows, width), F32),
            jax.ShapeDtypeStruct((1, width), F32),
        ),
        in_specs=[anywhere] * 8 + [smem, anywhere],
        out_specs=(vmem, vmem),
        scratch_shapes=[pltpu.VMEM(shape, dtype) for shape, dtype in scratch]
        + [
            pltpu.SemaphoreType.DMA((9,)),
            pltpu.SemaphoreType.DMA((18,)),
            pltpu.SemaphoreType.DMA((18,)),
        ],
        compiler_params=pltpu.CompilerParams(
            collective_id=0, has_side_effects=True, vmem_limit_bytes=60 * 1024 * 1024
        ),
    )(
        increment.reshape(half * rows, width),
        wind_u.reshape(half * rows, width),
        wind_v.reshape(half * rows, width),
        diffusion.reshape(1, half),
        mixing,
        jacobian,
        obs_weight.reshape(1, channels),
        innovation.reshape(32, channels, width),
        counts,
        column_lookup.reshape(16, width),
    )
    total_cells = increment.size * nlat * nlon * 2
    cost = lax.psum(jnp.sum(part), ("lat", "lon", "lev")) / total_cells
    return gradient.reshape(increment.shape), cost


def solution(mesh):
    field = P("lev", "lat", "lon")
    in_specs = (
        field,
        field,
        field,
        P("lev"),
        P("lev", None),
        P(None, "lev"),
        P(),
        P(None, "lat", "lon", None, None, None),
        P("lat", "lon"),
        P("lat", "lon", None),
    )
    return jax.shard_map(
        functools.partial(body, mesh.shape["lat"], mesh.shape["lon"]),
        mesh=mesh,
        in_specs=in_specs,
        out_specs=(field, P()),
        check_vma=False,
    )
```

time: 191 us -> 106 us (0.55)
  starting transfers between devices: 44.9 us -> 0 us
  local copies, waits for them, and re-layouts: 41.2 us -> 3.14 us
  Pallas kernels: 0 us -> 25 us
  waiting for transfers between devices: 15.2 us -> 0 us
  other arithmetic: 14.9 us -> 0.6 us
  blocking collectives: 63 us -> 74 us
  matrix products: 5.44 us -> 0 us
  between operations: 5.55 us -> 3.1 us
    ppermute x16 -> x0, starting transfers between devices: 33.2 us -> none  [the longest x8 32.3 us: with_halo(): lax.ppermute(leading, axis, [(b, a) for a, b in up])]
    gather x5 -> x0, local copies, waits for them, and re-layouts: 29.3 us -> none  [the longest x2 16 us: take_profiles(): selected_columns = jnp.take(state.reshape(level_count, -1), columns, axis=1)]
    psum x5 -> x1, blocking collectives: 46.1 us -> 74 us  [body(): cost = lax.psum(jnp.sum(part), ('lat', 'lon', 'lev')) / total_cells]
    pallas_call x0 -> x1, Pallas kernels: none -> 25 us  [body(): pl.pallas_call(functools.partial(kernel, (nlat, nlon, half, rows)), out_s...]
    ppermute x16 -> x0, waiting for transfers between devices: 15.2 us -> none  [the longest x8 8.48 us: with_halo(): lax.ppermute(last, axis, up)]
    all_to_all x3 -> x0, blocking collectives: 12.5 us -> none  [from_everyone(): return lax.all_to_all(copies, axis, split_axis=0, concat_axis=0, tiled=True)]
    all_to_all x3 -> x0, starting transfers between devices: 11.7 us -> none  [from_everyone(): return lax.all_to_all(copies, axis, split_axis=0, concat_axis=0, tiled=True)]
    dot_general x8 -> x0, matrix products: 5.44 us -> none  [the longest x2 2.48 us: body(): jnp.einsum('nl,slc->snc', jac_full, full_profiles, preferred_element_type...]
  transfers between devices with their start and end apart: 19 -> 0, of which waited for: 3 -> 0; matrix products, arithmetic and copies ran while one was open for 22% -> 0% of each run, Pallas kernels for 0% -> 0%
where the time goes in v1:
time: 106 us
  blocking collectives  74 us (70%)
  Pallas kernels  25 us (24%)
  local copies, waits for them, and re-layouts  3.14 us (3%)
  between operations  3.1 us (3%)
    psum x1, blocking collectives, body(): cost = lax.psum(jnp.sum(part), ('lat', 'lon', 'lev')) / total_cells  74 us
    pallas_call x1, Pallas kernels, body(): pl.pallas_call(functools.partial(kernel, (nlat, nlon, half, rows)), out_s...  25 us
    unnamed x6, local copies, waits for them, and re-layouts  3.14 us

profile of v1, /device:TPU:1, one launch (start us, length us, event | category | flops | bytes accessed | tf_op | source)
XLA Modules:
  0.0 105.8 jit_solution(13396864093869748933)
XLA Ops:
  0.6 0.0 copy-start
  1.3 0.0 copy-done
  1.3 0.7 copy.12.jac_h
  2.1 25.0 %shard_map.113 = (f32[640,128]{1,0:T(8,128)}, f32[1,128]{1,0:T(1,128)}) custom-call(f32[640,128]{1,0:T(8,128)} %bitcast.10, f32[640,128]{1,0:T(8,128)} %bitcast.11, f32[640,128]{1,0:T(8,128)} %bitcast.12, f32[1,40]{1,0:T(1,128)} %bitcast.14, f32[40,80]{1,0:T(8,128)} %mix_h.1, bf16[128,40]{1,0:T(8,128)(2,1)} %copy.12.jac_h, f32[1,128]{1,0:T(1,128)} %bitcast.15, ...), custom_call_target="tpu_custom_call" | custom-call | tf_op jit(solution)/shard_map/pallas_call | solution.py:428
  27.1 0.0 copy-start.1
  27.1 0.7 copy-done.1
  27.8 0.6 reduce_sum.9
  28.4 74.0 %psum.7 = f32[]{:T(128)} all-reduce(f32[]{:T(128)} %reduce_sum.9), channel_id=1, replica_groups=mesh['lat'=8,'lon'=16,'lev'=2] {'lat','lon','lev'}, use_global_device_ids=true, to_apply=%region_1.0 | all-reduce | flops 1 | bytes 8 | tf_op jit(solution)/shard_map/psum | solution.py:458
  103.0 1.7 %copy.15 = f32[40,16,128]{2,1,0:T(8,128)} copy(f32[40,16,128]{2,1,0:T(8,128)} %bitcast.9) | data formatting | bytes 655360
Async XLA Ops:
  0.6 0.7 copy-start
  27.1 0.7 copy-start.1

commit v2 on v1

--- a/solution.py
+++ b/solution.py
@@ -48,7 +48,7 @@
     south, north, south_in, north_in,
     strip_e, strip_w, strip_in, strip_s, strip_n,
     slots, pick, grid, grid_s, grid_n, edge, edge_in, edge_s, edge_n,
-    x0, x1, hu, hv, sm, f1, back, back_in,
+    x0, x1, hu, hv, sm, f1, hold, back, back_in, near, far,
     load_sem, send_sem, recv_sem,
 ):
     nlat, nlon, half, rows = sizes
@@ -62,6 +62,24 @@
     barrier = pltpu.get_barrier_semaphore()
     senders = [(up, j, h), (down, j, h), (i, j, other)]
     senders += [(a, side, k) for a in (i, up, down) for k in (0, 1)]
+    ring = nlon // 2 if nlon % 2 == 0 else nlon
+    laps = nlon // ring
+    crowd = nlat * laps * 2
+    lap, place_in_ring = lax.div(j, ring), lax.rem(j, ring)
+    me = (i * laps + lap) * 2 + h
+
+    def companion(t):
+        index = lax.rem(me + t, crowd)
+        return (
+            lax.div(index, 2 * laps),
+            lax.rem(lax.div(index, 2), laps) * ring + place_in_ring,
+            lax.rem(index, 2),
+        )
+
+    def follower(t):
+        return (i, lap * ring + lax.rem(place_in_ring + t, ring), h)
+
+    senders += [companion(t) for t in range(1, crowd)] + [follower(t) for t in range(1, ring)]
     for device in senders:
         pl.semaphore_signal(barrier, inc=1, device_id=device, device_id_type=MESH)
 
@@ -118,7 +136,7 @@
     misc[0] = jnp.zeros((half, LANES), F32)
     misc[0, :, 0:full_levels] = mix[...]
     eye = iota((half, half), 0) == iota((half, half), 1)
-    misc[1] = dot_nt(one_hot(eye), jac[...])
+    misc[1] = jac[...].astype(F32)
     column = jnp.sum(jnp.where(eye, dif[...], 0.0), axis=1, keepdims=True)
     misc[2] = jnp.broadcast_to(column, (half, LANES))
 
@@ -166,11 +184,12 @@
         full[n, there, :] = misc_in[n]
     mixing = full[0][:, 0:full_levels].astype(BF16)
     eye80 = one_hot(iota((full_levels, full_levels), 0) == iota((full_levels, full_levels), 1))
-    mixing_back = dot_nt(eye80, full[0].astype(BF16)[:, 0:full_levels]) if False else dot_tn(mixing, eye80)
-    mixing_back = mixing_back.astype(BF16)
+    mixing_back = dot_tn(mixing, eye80).astype(BF16)
     jac_t = full[1].astype(BF16)
     weighted = (full[1] * w_row).astype(BF16)
-    gram = dot_nt(weighted, jac_t).astype(BF16)
+    gram_full = dot_nt(weighted, jac_t)
+    gram = gram_full.astype(BF16)
+    gram = jnp.concatenate([gram, (gram_full - gram.astype(F32)).astype(BF16)], axis=1)
 
     for s in range(16):
         span = slice(LANES * s, LANES * (s + 1))
@@ -342,35 +361,67 @@
     f1[:, at_row(18)] = jnp.where(patched, value[:, at_row(0)], grid_n[:, at_row(0)].astype(F32))
     f1[:, at_row(19)] = grid_n[:, at_row(1)].astype(F32)
 
-    for pair in pairwise(1, 22):
+    def advance(pair):
         values = coupled(mixing, [step_row(x0, e) for e in pair])
         for e, value in zip(pair, values):
             x1[:, at_row(e)] = keep(e, value)
 
-    total = jnp.zeros((full_levels, LANES), F32)
-
-    def forced(states, pair, step, total):
+    def forced(states, pair, step):
         halves = [state.astype(BF16) for state in states]
-        image = dot(gram, jnp.concatenate(halves, axis=1))
-        result = []
+        joined = jnp.concatenate(halves, axis=1)
+        image = dot(gram, jnp.concatenate([joined, joined], axis=0))
+        result, parts = [], []
         for n, e in enumerate(pair):
             moved = f1[full_levels * step : full_levels * (step + 1), at_row(e - 2)]
             alive = f1[2 * full_levels : 2 * full_levels + 1, at_row(e - 2)]
             force = alive * image[:, at_row(n)] - moved
-            if HALO <= e < HALO + rows:
-                total = total + halves[n].astype(F32) * (force - moved)
+            parts.append(halves[n].astype(F32) * (force - moved))
             result.append(force)
-        return result, total
-
+        return result, sum(parts)
+
+    def force_first(pair):
+        forces, part = forced([x1[:, at_row(e)] for e in pair], pair, 0)
+        for e, force in zip(pair, forces):
+            hold[:, at_row(e)] = force
+        return part
+
+    def force_second(pair):
+        states = coupled(mixing, [step_row(x1, e) for e in pair])
+        forces, part = forced(states, pair, 1)
+        for e, force in zip(pair, forces):
+            sm[:, at_row(e)] = force
+        return part
+
+    inside = pairwise(HALO, HALO + rows - 1)
+    for pair in pairwise(3, 20):
+        advance(pair)
+    total = jnp.zeros((full_levels, LANES), F32)
+    for pair in inside:
+        total = total + force_first(pair)
+        total = total + force_second(pair)
+
+    increment = inc[...]
+    part = 0.5 * jnp.sum(increment * increment, axis=0, keepdims=True)
+    part = part + 0.25 * jnp.sum(squares, axis=0, keepdims=True)
+    part = part + 0.5 * jnp.sum(jnp.where(own_lanes, total, 0.0), axis=0, keepdims=True)
+    near[0] = part
+    first_round = [remote(18 + t, near.at[0], near.at[t], companion(t)) for t in range(1, crowd)]
+    for copy in first_round:
+        copy.start()
+
+    for pair in ((1, 2), (21, 22)):
+        advance(pair)
+    for pair in ((3,), (20,)):
+        force_first(pair)
+    for pair in ((2, 3), (20, 21)):
+        force_second(pair)
     for pair in pairwise(2, 21):
-        states = coupled(mixing, [step_row(x1, e) for e in pair])
-        forces, total = forced(states, pair, 1, total)
-        for e, value in zip(pair, coupled(mixing_back, forces)):
+        values = coupled(mixing_back, [sm[:, at_row(e)] for e in pair])
+        for e, value in zip(pair, values):
             x0[:, at_row(e)] = keep(e, value)
 
     for pair in pairwise(3, 20):
-        forces, total = forced([x1[:, at_row(e)] for e in pair], pair, 0, total)
-        values = [back_row(x0, e) + force for e, force in zip(pair, forces)]
+        values = [back_row(x0, e) + hold[:, at_row(e)] for e in pair]
         for e, value in zip(pair, coupled(mixing_back, values)):
             sm[:, at_row(e)] = keep(e, value)
 
@@ -381,11 +432,15 @@
     final = remote(17, back, back_in, (i, j, other))
     final.start()
 
-    increment = inc[...]
-    part = 0.5 * jnp.sum(increment * increment, axis=0, keepdims=True)
-    part = part + 0.25 * jnp.sum(squares, axis=0, keepdims=True)
-    part = part + 0.5 * jnp.sum(jnp.where(own_lanes, total, 0.0), axis=0, keepdims=True)
-    cost_ref[...] = part
+    for copy in first_round:
+        copy.wait_recv()
+    part = near[0]
+    for t in range(1, crowd):
+        part = part + near[t]
+    far[0] = part
+    second_round = [remote(18 + crowd + t, far.at[0], far.at[t], follower(t)) for t in range(1, ring)]
+    for copy in second_round:
+        copy.start()
 
     final.wait_recv()
     for q in range(rows // 2):
@@ -394,7 +449,14 @@
             r = 2 * q + t
             adjoint = jnp.where(own_lanes, x1[here, at_row(r)], received[half * t : half * (t + 1)])
             out_ref[pl.ds(r, half, stride=rows), :] = inc[pl.ds(r, half, stride=rows), :] + adjoint
-    for copy in copies + late + [relay_s, relay_n, final]:
+    for copy in second_round:
+        copy.wait_recv()
+    part = far[0]
+    for t in range(1, ring):
+        part = part + far[t]
+    cells = full_levels * rows * LANES * nlat * nlon
+    cost_ref[0, 0] = jnp.sum(part) / cells
+    for copy in copies + late + [relay_s, relay_n, final] + first_round + second_round:
         copy.wait_send()
 
 
@@ -408,10 +470,13 @@
     vmem = pl.BlockSpec(memory_space=pltpu.VMEM)
     smem = pl.BlockSpec(memory_space=pltpu.SMEM)
     grid_size = rows * width
+    far = nlon // 2 if nlon % 2 == 0 else nlon
+    near = nlat * (nlon // far) * 2
+    copies = 18 + near + far
     strip = (16, width)
     scratch = [
         ((half * rows, width), F32), ((half * rows, width), F32), ((half * rows, width), F32),
-        ((1, half), F32), ((half, levels), F32), ((channels, half), BF16), ((1, channels), F32),
+        ((1, half), F32), ((half, levels), F32), ((half, channels), BF16), ((1, channels), F32),
         ((32, channels, width), BF16), ((16, width), jnp.int32),
         ((3, 8, levels, width), BF16), ((3, 8, levels, width), BF16),
         ((3, half, width), F32), ((3, half, width), F32), ((3, levels, width), F32),
@@ -423,21 +488,22 @@
         ((16, 1024), BF16), ((16, 1024), BF16), ((16, 256), BF16), ((16, 256), BF16),
         ((levels, wide), F32), ((levels, wide), F32), ((levels, wide), F32), ((levels, wide), F32), ((levels, wide), F32),
         ((depth, 20 * width), F32),
-        ((8, levels, width), BF16), ((8, levels, width), BF16),
+        ((levels, wide), F32), ((8, levels, width), BF16), ((8, levels, width), BF16),
+        ((near, 1, width), F32), ((far, 1, width), F32),
     ]
-    gradient, part = pl.pallas_call(
+    gradient, cost = pl.pallas_call(
         functools.partial(kernel, (nlat, nlon, half, rows)),
         out_shape=(
             jax.ShapeDtypeStruct((half * rows, width), F32),
-            jax.ShapeDtypeStruct((1, width), F32),
+            jax.ShapeDtypeStruct((1, 1), F32),
         ),
         in_specs=[anywhere] * 8 + [smem, anywhere],
-        out_specs=(vmem, vmem),
+        out_specs=(vmem, smem),
         scratch_shapes=[pltpu.VMEM(shape, dtype) for shape, dtype in scratch]
         + [
             pltpu.SemaphoreType.DMA((9,)),
-            pltpu.SemaphoreType.DMA((18,)),
-            pltpu.SemaphoreType.DMA((18,)),
+            pltpu.SemaphoreType.DMA((copies,)),
+            pltpu.SemaphoreType.DMA((copies,)),
         ],
         compiler_params=pltpu.CompilerParams(
             collective_id=0, has_side_effects=True, vmem_limit_bytes=60 * 1024 * 1024
@@ -448,15 +514,13 @@
         wind_v.reshape(half * rows, width),
         diffusion.reshape(1, half),
         mixing,
-        jacobian,
+        jacobian.T,
         obs_weight.reshape(1, channels),
         innovation.reshape(32, channels, width),
         counts,
         column_lookup.reshape(16, width),
     )
-    total_cells = increment.size * nlat * nlon * 2
-    cost = lax.psum(jnp.sum(part), ("lat", "lon", "lev")) / total_cells
-    return gradient.reshape(increment.shape), cost
+    return gradient.reshape(increment.shape), cost.reshape(())
 
 
 def solution(mesh):

time: 106 us -> 37.3 us (0.35)
  blocking collectives: 74 us -> 0 us
  Pallas kernels: 25 us -> 32.5 us
  local copies, waits for them, and re-layouts: 3.14 us -> 1.72 us
    psum x1 -> x0, blocking collectives: 74 us -> none  [body(): cost = lax.psum(jnp.sum(part), ('lat', 'lon', 'lev')) / total_cells]
    pallas_call x1, Pallas kernels: 25 us -> 32.5 us  [body(): pl.pallas_call(functools.partial(kernel, (nlat, nlon, half, rows)), out_s...]
    unnamed x6 -> x1, local copies, waits for them, and re-layouts: 3.14 us -> 1.72 us
where the time goes in v2:
time: 37.3 us; the launch traced here: 37.2 us
  Pallas kernels  32.5 us (87%)
  between operations  2.98 us (8%)
  local copies, waits for them, and re-layouts  1.72 us (5%)
    pallas_call x1, Pallas kernels, body(): pl.pallas_call(functools.partial(kernel, (nlat, nlon, half, rows)), out_s...  32.5 us
    unnamed x1, local copies, waits for them, and re-layouts  1.72 us

profile of v2, /device:TPU:1, one launch (start us, length us, event | category | flops | bytes accessed | tf_op | source)
XLA Modules:
  0.0 37.2 jit_solution(13742657923073948248)
XLA Ops:
  1.3 32.5 %shard_map.113 = (f32[640,128]{1,0:T(8,128)}, f32[1,1]{1,0:T(1,128)}) custom-call(f32[640,128]{1,0:T(8,128)} %bitcast.11, f32[640,128]{1,0:T(8,128)} %bitcast.12, f32[640,128]{1,0:T(8,128)} %bitcast.13, f32[1,40]{1,0:T(1,128)} %bitcast.17, f32[40,80]{1,0:T(8,128)} %mix_h.1, bf16[40,128]{1,0:T(8,128)(2,1)} %bitcast.15, f32[1,128]{1,0:T(1,128)} %bitcast.18, ...), custom_call_target="tpu_custom_call" | custom-call | tf_op jit(solution)/shard_map/pallas_call | solution.py:494
  33.8 1.7 %copy.15 = f32[40,16,128]{2,1,0:T(8,128)} copy(f32[40,16,128]{2,1,0:T(8,128)} %bitcast.14) | data formatting | bytes 655360

commit v3 on v2

--- a/solution.py
+++ b/solution.py
@@ -41,7 +41,7 @@
 
 def kernel(
     sizes,
-    inc_h, u_h, v_h, dif_h, mix_h, jac_h, w_h, y_h, cnt_s, lut_h,
+    inc_h, u_h, v_h, dif_h, mix_h, jac_h, w_h, y_h, lut_h, cnt,
     out_ref, cost_ref,
     inc, u, v, dif, mix, jac, w, y, lut,
     own, partner, misc, misc_in, full,
@@ -109,7 +109,7 @@
 
     for q in range(rows // 2):
         for f in range(3):
-            own[f, q] = jnp.concatenate([own_row(f, 2 * q), own_row(f, 2 * q + 1)], axis=0).astype(BF16)
+            own[q, f] = jnp.concatenate([own_row(f, 2 * q), own_row(f, 2 * q + 1)], axis=0).astype(BF16)
 
     wide = (32, 3 * LANES)
     number, lane = iota(wide, 0), iota(wide, 1)
@@ -140,23 +140,6 @@
     column = jnp.sum(jnp.where(eye, dif[...], 0.0), axis=1, keepdims=True)
     misc[2] = jnp.broadcast_to(column, (half, LANES))
 
-    pl.semaphore_wait(barrier, len(senders))
-
-    copies = [
-        remote(2, own.at[:, 6:8], south, (up, j, h)),
-        remote(3, own.at[:, 0:2], north, (down, j, h)),
-        remote(6, strip_e, strip_in.at[h], (i, east, 0), 6 + h),
-        remote(7, strip_w, strip_in.at[h], (i, west, 1), 6 + h),
-        remote(8, strip_e.at[5], strip_s.at[h], (up, east, 0), 8 + h),
-        remote(9, strip_e.at[0], strip_n.at[h], (down, east, 0), 10 + h),
-        remote(10, strip_w.at[5], strip_s.at[h], (up, west, 1), 8 + h),
-        remote(11, strip_w.at[0], strip_n.at[h], (down, west, 1), 10 + h),
-        remote(1, misc, misc_in, (i, j, other)),
-        remote(0, own, partner, (i, j, other)),
-    ]
-    for copy in copies:
-        copy.start()
-
     table = lut[...]
     low = dot_nt(one_hot(iota((LANES, LANES), 0) == iota((LANES, LANES), 1)), (table & 255).astype(F32).astype(BF16))
     pair_lane = iota((LANES, 2 * LANES), 1).astype(F32)
@@ -164,7 +147,7 @@
         pick[LANES * s : LANES * (s + 1)] = one_hot(jnp.broadcast_to(low[:, s : s + 1], (LANES, 2 * LANES)) == pair_lane)
     pair_of = (table >> 8).astype(F32)
 
-    count = cnt_s[0, 0]
+    count = cnt[...]
     live = [jnp.where(count > s, 1.0, 0.0).astype(F32) for s in range(16)]
     loads[8].wait()
     w_row = w[...]
@@ -177,7 +160,31 @@
         squares = squares + live[s] * (first * first + second * second)
     squares = squares * w_column
 
-    copies[8].wait_recv()
+    increment = inc[...]
+    known = 0.5 * jnp.sum(increment * increment, axis=0, keepdims=True)
+    known = known + 0.25 * jnp.sum(squares, axis=0, keepdims=True)
+
+    pl.semaphore_wait(barrier, len(senders))
+
+    copies = [
+        remote(8, strip_e.at[5], strip_s.at[h], (up, east, 0), 8 + h),
+        remote(9, strip_e.at[0], strip_n.at[h], (down, east, 0), 10 + h),
+        remote(10, strip_w.at[5], strip_s.at[h], (up, west, 1), 8 + h),
+        remote(11, strip_w.at[0], strip_n.at[h], (down, west, 1), 10 + h),
+        remote(2, own.at[7], south.at[1], (up, j, h)),
+        remote(3, own.at[0], north.at[0], (down, j, h)),
+        remote(6, strip_e, strip_in.at[h], (i, east, 0), 6 + h),
+        remote(7, strip_w, strip_in.at[h], (i, west, 1), 6 + h),
+        remote(1, misc, misc_in, (i, j, other)),
+        remote(0, own, partner, (i, j, other)),
+        remote(17, own.at[6], south.at[0], (up, j, h)),
+        remote(18, own.at[1], north.at[1], (down, j, h)),
+    ]
+    near_s, near_n, misc_copy, own_copy, far_s, far_n = copies[4], copies[5], copies[8], copies[9], copies[10], copies[11]
+    for copy in copies:
+        copy.start()
+
+    misc_copy.wait_recv()
     here, there = pl.ds(pl.multiple_of(h * half, 8), half), pl.ds(pl.multiple_of(other * half, 8), half)
     for n in range(3):
         full[n, here, :] = misc[n]
@@ -229,12 +236,12 @@
     for copy in late:
         copy.start()
 
-    copies[0].wait_recv()
-    relay_s = remote(4, south, south_in, (i, j, other))
-    relay_s.start()
-    copies[1].wait_recv()
-    relay_n = remote(5, north, north_in, (i, j, other))
-    relay_n.start()
+    near_s.wait_recv()
+    relays = [remote(4, south.at[1], south_in.at[1], (i, j, other))]
+    relays[0].start()
+    near_n.wait_recv()
+    relays.append(remote(5, north.at[0], north_in.at[0], (i, j, other)))
+    relays[1].start()
 
     lane_row = iota((1, LANES), 1)
     patched = jnp.where(h == 0, lane_row - (LANES - HALO), HALO - 1 - lane_row) >= 0
@@ -262,13 +269,13 @@
                 targets[f][span, at_row(e)] = keep(e, value)
 
     def rows_of(ref, q):
-        blocks = [ref[f, q].astype(F32) for f in range(3)]
+        blocks = [ref[q, f].astype(F32) for f in range(3)]
         return [[block[half * t : half * (t + 1)] for block in blocks] for t in (0, 1)]
 
     def patch_of(ref):
         return dot_tn(ref[:, 0 : 3 * half], place)
 
-    copies[9].wait_recv()
+    own_copy.wait_recv()
     for k in (0, 1):
         remote(6, strip_e, strip_in.at[k], (i, east, 0), 6 + k).wait_recv()
     group_of = {}
@@ -293,26 +300,6 @@
         for t in (0, 1):
             r = 2 * q + t
             assemble(HALO + r, (mine[t], theirs[t]), patches_for(r))
-    relay_s.wait_recv()
-    relay_n.wait_recv()
-    for k in (0, 1):
-        remote(8, strip_e.at[5], strip_s.at[k], (i, east, 0), 8 + k).wait_recv()
-        remote(9, strip_e.at[0], strip_n.at[k], (i, east, 0), 10 + k).wait_recv()
-    patch = (patch_of(strip_s.at[h]), patch_of(strip_s.at[other]))
-    for q in (0, 1):
-        mine, theirs = rows_of(south, q), rows_of(south_in, q)
-        for t in (0, 1):
-            e = 2 * q + t
-            fit = [None if e == 0 else value[half * (e - 1) : half * e] for value in patch]
-            assemble(e, (mine[t], theirs[t]), fit)
-    patch = (patch_of(strip_n.at[h]), patch_of(strip_n.at[other]))
-    for q in (0, 1):
-        mine, theirs = rows_of(north, q), rows_of(north_in, q)
-        for t in (0, 1):
-            e = 2 * q + t
-            fit = [None if e == 3 else value[half * e : half * (e + 1)] for value in patch]
-            assemble(HALO + rows + e, (mine[t], theirs[t]), fit)
-
     diffusion = full[2]
     centre = 1.0 - 4.0 * diffusion
 
@@ -347,6 +334,80 @@
     def pairwise(first, last):
         return [tuple(range(e, min(e + 2, last + 1))) for e in range(first, last + 1, 2)]
 
+    def advance(pair):
+        values = coupled(mixing, [step_row(x0, e) for e in pair])
+        for e, value in zip(pair, values):
+            x1[:, at_row(e)] = keep(e, value)
+
+    def image_of(states, pair, target):
+        halves = [state.astype(BF16) for state in states]
+        joined = jnp.concatenate(halves, axis=1)
+        image = dot(gram, jnp.concatenate([joined, joined], axis=0))
+        for n, e in enumerate(pair):
+            target[:, at_row(e)] = image[:, at_row(n)]
+        return halves
+
+    def misfit(halves, pair, target, step):
+        parts = []
+        for half_state, e in zip(halves, pair):
+            r = e - HALO
+            moved = grid[full_levels * step : full_levels * (step + 1), at_row(r)].astype(F32)
+            alive = grid[2 * full_levels : depth, at_row(r)].astype(F32)[0:1]
+            parts.append(half_state.astype(F32) * (alive * target[:, at_row(e)] - 2.0 * moved))
+        return sum(parts)
+
+    def image_first(pair):
+        return image_of([x1[:, at_row(e)] for e in pair], pair, hold)
+
+    def image_second(pair):
+        return image_of(coupled(mixing, [step_row(x1, e) for e in pair]), pair, sm)
+
+    for pair in pairwise(5, 18):
+        advance(pair)
+    total = jnp.zeros((full_levels, LANES), F32)
+    for pair in pairwise(6, 17):
+        total = total + misfit(image_first(pair), pair, hold, 0)
+        total = total + misfit(image_second(pair), pair, sm, 1)
+
+    for copy in relays:
+        copy.wait_recv()
+    for k in (0, 1):
+        remote(8, strip_e.at[5], strip_s.at[k], (i, east, 0), 8 + k).wait_recv()
+        remote(9, strip_e.at[0], strip_n.at[k], (i, east, 0), 10 + k).wait_recv()
+    patch_s = (patch_of(strip_s.at[h]), patch_of(strip_s.at[other]))
+    patch_n = (patch_of(strip_n.at[h]), patch_of(strip_n.at[other]))
+
+    def outer_rows(which):
+        q = 1 - which
+        mine, theirs = rows_of(south, q), rows_of(south_in, q)
+        for t in (0, 1):
+            e = 2 * q + t
+            fit = [None if e == 0 else value[half * (e - 1) : half * e] for value in patch_s]
+            assemble(e, (mine[t], theirs[t]), fit)
+        q = which
+        mine, theirs = rows_of(north, q), rows_of(north_in, q)
+        for t in (0, 1):
+            e = 2 * q + t
+            fit = [None if e == 3 else value[half * e : half * (e + 1)] for value in patch_n]
+            assemble(HALO + rows + e, (mine[t], theirs[t]), fit)
+
+    outer_rows(0)
+    for pair in ((3, 4), (19, 20)):
+        advance(pair)
+    for pair in ((4, 5), (18, 19)):
+        total = total + misfit(image_first(pair), pair, hold, 0)
+        total = total + misfit(image_second(pair), pair, sm, 1)
+    near[0] = known + 0.5 * jnp.sum(jnp.where(own_lanes, total, 0.0), axis=0, keepdims=True)
+    first_round = [remote(21 + t, near.at[0], near.at[t], companion(t)) for t in range(1, crowd)]
+    for copy in first_round:
+        copy.start()
+
+    far_s.wait_recv()
+    relays.append(remote(19, south.at[0], south_in.at[0], (i, j, other)))
+    relays[2].start()
+    far_n.wait_recv()
+    relays.append(remote(20, north.at[1], north_in.at[1], (i, j, other)))
+    relays[3].start()
     for copy in late:
         copy.wait_recv()
     for q in range(4):
@@ -361,67 +422,28 @@
     f1[:, at_row(18)] = jnp.where(patched, value[:, at_row(0)], grid_n[:, at_row(0)].astype(F32))
     f1[:, at_row(19)] = grid_n[:, at_row(1)].astype(F32)
 
-    def advance(pair):
-        values = coupled(mixing, [step_row(x0, e) for e in pair])
-        for e, value in zip(pair, values):
-            x1[:, at_row(e)] = keep(e, value)
-
-    def forced(states, pair, step):
-        halves = [state.astype(BF16) for state in states]
-        joined = jnp.concatenate(halves, axis=1)
-        image = dot(gram, jnp.concatenate([joined, joined], axis=0))
-        result, parts = [], []
-        for n, e in enumerate(pair):
-            moved = f1[full_levels * step : full_levels * (step + 1), at_row(e - 2)]
-            alive = f1[2 * full_levels : 2 * full_levels + 1, at_row(e - 2)]
-            force = alive * image[:, at_row(n)] - moved
-            parts.append(halves[n].astype(F32) * (force - moved))
-            result.append(force)
-        return result, sum(parts)
-
-    def force_first(pair):
-        forces, part = forced([x1[:, at_row(e)] for e in pair], pair, 0)
-        for e, force in zip(pair, forces):
-            hold[:, at_row(e)] = force
-        return part
-
-    def force_second(pair):
-        states = coupled(mixing, [step_row(x1, e) for e in pair])
-        forces, part = forced(states, pair, 1)
-        for e, force in zip(pair, forces):
-            sm[:, at_row(e)] = force
-        return part
-
-    inside = pairwise(HALO, HALO + rows - 1)
-    for pair in pairwise(3, 20):
-        advance(pair)
-    total = jnp.zeros((full_levels, LANES), F32)
-    for pair in inside:
-        total = total + force_first(pair)
-        total = total + force_second(pair)
-
-    increment = inc[...]
-    part = 0.5 * jnp.sum(increment * increment, axis=0, keepdims=True)
-    part = part + 0.25 * jnp.sum(squares, axis=0, keepdims=True)
-    part = part + 0.5 * jnp.sum(jnp.where(own_lanes, total, 0.0), axis=0, keepdims=True)
-    near[0] = part
-    first_round = [remote(18 + t, near.at[0], near.at[t], companion(t)) for t in range(1, crowd)]
-    for copy in first_round:
-        copy.start()
-
+    for copy in relays[2:]:
+        copy.wait_recv()
+    outer_rows(1)
     for pair in ((1, 2), (21, 22)):
         advance(pair)
     for pair in ((3,), (20,)):
-        force_first(pair)
+        image_first(pair)
     for pair in ((2, 3), (20, 21)):
-        force_second(pair)
+        image_second(pair)
+
+    def force(e, target, step):
+        moved = f1[full_levels * step : full_levels * (step + 1), at_row(e - 2)]
+        alive = f1[2 * full_levels : 2 * full_levels + 1, at_row(e - 2)]
+        return alive * target[:, at_row(e)] - moved
+
     for pair in pairwise(2, 21):
-        values = coupled(mixing_back, [sm[:, at_row(e)] for e in pair])
+        values = coupled(mixing_back, [force(e, sm, 1) for e in pair])
         for e, value in zip(pair, values):
             x0[:, at_row(e)] = keep(e, value)
 
     for pair in pairwise(3, 20):
-        values = [back_row(x0, e) + hold[:, at_row(e)] for e in pair]
+        values = [back_row(x0, e) + force(e, hold, 0) for e in pair]
         for e, value in zip(pair, coupled(mixing_back, values)):
             sm[:, at_row(e)] = keep(e, value)
 
@@ -429,7 +451,7 @@
         x1[:, at_row(r)] = back_row(sm, r + HALO)
     for q in range(rows // 2):
         back[q] = jnp.concatenate([x1[there, at_row(2 * q)], x1[there, at_row(2 * q + 1)]], axis=0).astype(BF16)
-    final = remote(17, back, back_in, (i, j, other))
+    final = remote(21, back, back_in, (i, j, other))
     final.start()
 
     for copy in first_round:
@@ -438,7 +460,7 @@
     for t in range(1, crowd):
         part = part + near[t]
     far[0] = part
-    second_round = [remote(18 + crowd + t, far.at[0], far.at[t], follower(t)) for t in range(1, ring)]
+    second_round = [remote(21 + crowd + t, far.at[0], far.at[t], follower(t)) for t in range(1, ring)]
     for copy in second_round:
         copy.start()
 
@@ -456,8 +478,15 @@
         part = part + far[t]
     cells = full_levels * rows * LANES * nlat * nlon
     cost_ref[0, 0] = jnp.sum(part) / cells
-    for copy in copies + late + [relay_s, relay_n, final] + first_round + second_round:
+    for copy in copies + late + relays + [final] + first_round + second_round:
         copy.wait_send()
+
+
+def deliver(gradient, cost, gradient_out, cost_out, sem):
+    copy = pltpu.make_async_copy(gradient, gradient_out, sem)
+    copy.start()
+    cost_out[0, 0] = cost[0, 0]
+    copy.wait()
 
 
 def body(nlat, nlon, increment, wind_u, wind_v, diffusion, mixing, jacobian, obs_weight, innovation, counts, column_lookup):
@@ -466,22 +495,22 @@
     wide = (HALO * 2 + rows) * width
     levels = 2 * half
     depth = 2 * levels + 16
-    anywhere = pl.BlockSpec(memory_space=pl.ANY)
+    anywhere = pl.BlockSpec(memory_space=pltpu.MemorySpace.HBM)
     vmem = pl.BlockSpec(memory_space=pltpu.VMEM)
     smem = pl.BlockSpec(memory_space=pltpu.SMEM)
     grid_size = rows * width
     far = nlon // 2 if nlon % 2 == 0 else nlon
     near = nlat * (nlon // far) * 2
-    copies = 18 + near + far
+    copies = 21 + near + far
     strip = (16, width)
     scratch = [
         ((half * rows, width), F32), ((half * rows, width), F32), ((half * rows, width), F32),
         ((1, half), F32), ((half, levels), F32), ((half, channels), BF16), ((1, channels), F32),
         ((32, channels, width), BF16), ((16, width), jnp.int32),
-        ((3, 8, levels, width), BF16), ((3, 8, levels, width), BF16),
+        ((8, 3, levels, width), BF16), ((8, 3, levels, width), BF16),
         ((3, half, width), F32), ((3, half, width), F32), ((3, levels, width), F32),
-        ((3, 2, levels, width), BF16), ((3, 2, levels, width), BF16),
-        ((3, 2, levels, width), BF16), ((3, 2, levels, width), BF16),
+        ((2, 3, levels, width), BF16), ((2, 3, levels, width), BF16),
+        ((2, 3, levels, width), BF16), ((2, 3, levels, width), BF16),
         ((6, *strip), BF16), ((6, *strip), BF16), ((2, 6, *strip), BF16), ((2, *strip), BF16), ((2, *strip), BF16),
         ((depth, grid_size), BF16), ((grid_size, 2 * width), BF16), ((depth, grid_size), BF16),
         ((depth, 2 * width), BF16), ((depth, 2 * width), BF16),
@@ -497,29 +526,45 @@
             jax.ShapeDtypeStruct((half * rows, width), F32),
             jax.ShapeDtypeStruct((1, 1), F32),
         ),
-        in_specs=[anywhere] * 8 + [smem, anywhere],
+        in_specs=[anywhere] * 9 + [vmem],
         out_specs=(vmem, smem),
-        scratch_shapes=[pltpu.VMEM(shape, dtype) for shape, dtype in scratch]
+        scratch_shapes=[pltpu.VMEM(*entry) for entry in scratch]
         + [
             pltpu.SemaphoreType.DMA((9,)),
             pltpu.SemaphoreType.DMA((copies,)),
             pltpu.SemaphoreType.DMA((copies,)),
         ],
         compiler_params=pltpu.CompilerParams(
-            collective_id=0, has_side_effects=True, vmem_limit_bytes=60 * 1024 * 1024
+            collective_id=0, has_side_effects=True, vmem_limit_bytes=24 * 1024 * 1024
         ),
     )(
-        increment.reshape(half * rows, width),
-        wind_u.reshape(half * rows, width),
-        wind_v.reshape(half * rows, width),
-        diffusion.reshape(1, half),
-        mixing,
-        jacobian.T,
-        obs_weight.reshape(1, channels),
-        innovation.reshape(32, channels, width),
+        *[
+            pltpu.with_memory_space_constraint(operand, pltpu.MemorySpace.HBM)
+            for operand in (
+                increment.reshape(half * rows, width),
+                wind_u.reshape(half * rows, width),
+                wind_v.reshape(half * rows, width),
+                diffusion.reshape(1, half),
+                mixing,
+                jacobian.T,
+                obs_weight.reshape(1, channels),
+                innovation.reshape(32, channels, width),
+                column_lookup.reshape(16, width),
+            )
+        ],
         counts,
-        column_lookup.reshape(16, width),
     )
+    gradient, cost = pl.pallas_call(
+        deliver,
+        out_shape=(
+            jax.ShapeDtypeStruct((half * rows, width), F32),
+            jax.ShapeDtypeStruct((1, 1), F32),
+        ),
+        in_specs=[vmem, smem],
+        out_specs=(pl.BlockSpec(memory_space=pl.ANY), smem),
+        scratch_shapes=[pltpu.SemaphoreType.DMA],
+        compiler_params=pltpu.CompilerParams(vmem_limit_bytes=1024 * 1024),
+    )(gradient, cost)
     return gradient.reshape(increment.shape), cost.reshape(())
 
 

time: 37.3 us -> 33 us (0.88)
  local copies, waits for them, and re-layouts: 1.72 us -> 0 us
  between operations: 2.98 us -> 1.29 us
  Pallas kernels: 32.5 us -> 31.6 us
    pallas_call x1, Pallas kernels: 32.5 us -> 29.7 us  [body(): pl.pallas_call(functools.partial(kernel, (nlat, nlon, half, rows)), out_s...]
    pallas_call x0 -> x1, Pallas kernels: none -> 1.88 us  [body(): pl.pallas_call(deliver, out_shape=(jax.ShapeDtypeStruct((half * rows, wid...]
    unnamed x1 -> x0, local copies, waits for them, and re-layouts: 1.72 us -> none
where the time goes in v3:
time: 33 us; the launch traced here: 32.8 us
  Pallas kernels  31.6 us (96%)
  between operations  1.29 us (4%)
    pallas_call x1, Pallas kernels, body(): pl.pallas_call(functools.partial(kernel, (nlat, nlon, half, rows)), out_s...  29.7 us
    pallas_call x1, Pallas kernels, body(): pl.pallas_call(deliver, out_shape=(jax.ShapeDtypeStruct((half * rows, wid...  1.88 us

profile of v3, /device:TPU:1, one launch (start us, length us, event | category | flops | bytes accessed | tf_op | source)
XLA Modules:
  0.0 32.8 jit_solution(5735272113995215845)
XLA Ops:
  1.3 29.7 %shard_map.113 = (f32[640,128]{1,0:T(8,128)S(1)}, f32[1,1]{1,0:T(1,128)}) custom-call(f32[640,128]{1,0:T(8,128)} %bitcast.11, f32[640,128]{1,0:T(8,128)} %bitcast.12, f32[640,128]{1,0:T(8,128)} %bitcast.13, f32[1,40]{1,0:T(1,128)} %bitcast.16, f32[40,80]{1,0:T(8,128)} %mix_h.1, bf16[40,128]{1,0:T(8,128)(2,1)} %bitcast.14, f32[1,128]{1,0:T(1,128)} %bitcast.17, ...), custom_call_target="tpu_custom_call" | custom-call | tf_op jit(solution)/shard_map/pallas_call | solution.py:523
  31.0 1.9 %shard_map.114 = (f32[640,128]{1,0:T(8,128)}, f32[1,1]{1,0:T(1,128)}) custom-call(f32[640,128]{1,0:T(8,128)S(1)} %get-tuple-element.6.gradient, f32[1,1]{1,0:T(1,128)} %get-tuple-element.7.cost), custom_call_target="tpu_custom_call" | custom-call | tf_op jit(solution)/shard_map/pallas_call | solution.py:557

commit v4 on v3

--- a/solution.py
+++ b/solution.py
@@ -59,6 +59,12 @@
     east, west = lax.rem(j + 1, nlon), lax.rem(j + nlon - 1, nlon)
     side = lax.rem(j + nlon - 1 + 2 * h, nlon)
 
+    loads = {}
+    pairs = ((inc_h, inc), (u_h, u), (v_h, v), (dif_h, dif), (mix_h, mix), (jac_h, jac), (w_h, w), (lut_h, lut), (y_h, y))
+    for n, (source, target) in enumerate(pairs):
+        loads[n] = pltpu.make_async_copy(source, target, load_sem.at[n])
+        loads[n].start()
+
     barrier = pltpu.get_barrier_semaphore()
     senders = [(up, j, h), (down, j, h), (i, j, other)]
     senders += [(a, side, k) for a in (i, up, down) for k in (0, 1)]
@@ -82,12 +88,6 @@
     senders += [companion(t) for t in range(1, crowd)] + [follower(t) for t in range(1, ring)]
     for device in senders:
         pl.semaphore_signal(barrier, inc=1, device_id=device, device_id_type=MESH)
-
-    loads = {}
-    pairs = ((inc_h, inc), (u_h, u), (v_h, v), (dif_h, dif), (mix_h, mix), (jac_h, jac), (w_h, w), (lut_h, lut), (y_h, y))
-    for n, (source, target) in enumerate(pairs):
-        loads[n] = pltpu.make_async_copy(source, target, load_sem.at[n])
-        loads[n].start()
 
     def remote(n, source, target, device, arrival=None):
         return pltpu.make_async_remote_copy(
@@ -107,9 +107,17 @@
         value = fields[f][pl.ds(r, half, stride=rows), :]
         return value if f == 0 else 0.5 * value
 
-    for q in range(rows // 2):
+    def pack(q):
         for f in range(3):
             own[q, f] = jnp.concatenate([own_row(f, 2 * q), own_row(f, 2 * q + 1)], axis=0).astype(BF16)
+
+    pack(7)
+    pack(0)
+    pl.semaphore_wait(barrier, len(senders))
+    near_s = remote(2, own.at[7], south.at[1], (up, j, h))
+    near_n = remote(3, own.at[0], north.at[0], (down, j, h))
+    near_s.start()
+    near_n.start()
 
     wide = (32, 3 * LANES)
     number, lane = iota(wide, 0), iota(wide, 1)
@@ -131,6 +139,17 @@
         strip_e[g, :, 3 * half : LANES] = jnp.zeros((16, LANES - 3 * half), BF16)
         strip_w[g, :, 3 * half : LANES] = jnp.zeros((16, LANES - 3 * half), BF16)
 
+    copies = [
+        remote(8, strip_e.at[5], strip_s.at[h], (up, east, 0), 8 + h),
+        remote(9, strip_e.at[0], strip_n.at[h], (down, east, 0), 10 + h),
+        remote(10, strip_w.at[5], strip_s.at[h], (up, west, 1), 8 + h),
+        remote(11, strip_w.at[0], strip_n.at[h], (down, west, 1), 10 + h),
+        remote(6, strip_e, strip_in.at[h], (i, east, 0), 6 + h),
+        remote(7, strip_w, strip_in.at[h], (i, west, 1), 6 + h),
+    ]
+    for copy in copies:
+        copy.start()
+
     for n in range(3, 8):
         loads[n].wait()
     misc[0] = jnp.zeros((half, LANES), F32)
@@ -139,6 +158,17 @@
     misc[1] = jac[...].astype(F32)
     column = jnp.sum(jnp.where(eye, dif[...], 0.0), axis=1, keepdims=True)
     misc[2] = jnp.broadcast_to(column, (half, LANES))
+    misc_copy = remote(1, misc, misc_in, (i, j, other))
+    misc_copy.start()
+    for q in range(1, 7):
+        pack(q)
+    own_copy = remote(0, own, partner, (i, j, other))
+    far_s = remote(17, own.at[6], south.at[0], (up, j, h))
+    far_n = remote(18, own.at[1], north.at[1], (down, j, h))
+    own_copy.start()
+    far_s.start()
+    far_n.start()
+    copies += [near_s, near_n, misc_copy, own_copy, far_s, far_n]
 
     table = lut[...]
     low = dot_nt(one_hot(iota((LANES, LANES), 0) == iota((LANES, LANES), 1)), (table & 255).astype(F32).astype(BF16))
@@ -163,26 +193,6 @@
     increment = inc[...]
     known = 0.5 * jnp.sum(increment * increment, axis=0, keepdims=True)
     known = known + 0.25 * jnp.sum(squares, axis=0, keepdims=True)
-
-    pl.semaphore_wait(barrier, len(senders))
-
-    copies = [
-        remote(8, strip_e.at[5], strip_s.at[h], (up, east, 0), 8 + h),
-        remote(9, strip_e.at[0], strip_n.at[h], (down, east, 0), 10 + h),
-        remote(10, strip_w.at[5], strip_s.at[h], (up, west, 1), 8 + h),
-        remote(11, strip_w.at[0], strip_n.at[h], (down, west, 1), 10 + h),
-        remote(2, own.at[7], south.at[1], (up, j, h)),
-        remote(3, own.at[0], north.at[0], (down, j, h)),
-        remote(6, strip_e, strip_in.at[h], (i, east, 0), 6 + h),
-        remote(7, strip_w, strip_in.at[h], (i, west, 1), 6 + h),
-        remote(1, misc, misc_in, (i, j, other)),
-        remote(0, own, partner, (i, j, other)),
-        remote(17, own.at[6], south.at[0], (up, j, h)),
-        remote(18, own.at[1], north.at[1], (down, j, h)),
-    ]
-    near_s, near_n, misc_copy, own_copy, far_s, far_n = copies[4], copies[5], copies[8], copies[9], copies[10], copies[11]
-    for copy in copies:
-        copy.start()
 
     misc_copy.wait_recv()
     here, there = pl.ds(pl.multiple_of(h * half, 8), half), pl.ds(pl.multiple_of(other * half, 8), half)
@@ -477,16 +487,21 @@
     for t in range(1, ring):
         part = part + far[t]
     cells = full_levels * rows * LANES * nlat * nlon
-    cost_ref[0, 0] = jnp.sum(part) / cells
+    cost_ref[...] = jnp.broadcast_to(jnp.sum(part, axis=1, keepdims=True) * (1.0 / cells), (1, LANES))
     for copy in copies + late + relays + [final] + first_round + second_round:
         copy.wait_send()
 
 
-def deliver(gradient, cost, gradient_out, cost_out, sem):
-    copy = pltpu.make_async_copy(gradient, gradient_out, sem)
-    copy.start()
-    cost_out[0, 0] = cost[0, 0]
-    copy.wait()
+def deliver(gradient, cost, gradient_out, cost_out, single, sem):
+    single[...] = cost[:, 0:1]
+    copies = (
+        pltpu.make_async_copy(gradient, gradient_out, sem.at[0]),
+        pltpu.make_async_copy(single, cost_out, sem.at[1]),
+    )
+    for copy in copies:
+        copy.start()
+    for copy in copies:
+        copy.wait()
 
 
 def body(nlat, nlon, increment, wind_u, wind_v, diffusion, mixing, jacobian, obs_weight, innovation, counts, column_lookup):
@@ -497,7 +512,6 @@
     depth = 2 * levels + 16
     anywhere = pl.BlockSpec(memory_space=pltpu.MemorySpace.HBM)
     vmem = pl.BlockSpec(memory_space=pltpu.VMEM)
-    smem = pl.BlockSpec(memory_space=pltpu.SMEM)
     grid_size = rows * width
     far = nlon // 2 if nlon % 2 == 0 else nlon
     near = nlat * (nlon // far) * 2
@@ -524,10 +538,10 @@
         functools.partial(kernel, (nlat, nlon, half, rows)),
         out_shape=(
             jax.ShapeDtypeStruct((half * rows, width), F32),
-            jax.ShapeDtypeStruct((1, 1), F32),
+            jax.ShapeDtypeStruct((1, width), F32),
         ),
         in_specs=[anywhere] * 9 + [vmem],
-        out_specs=(vmem, smem),
+        out_specs=(vmem, vmem),
         scratch_shapes=[pltpu.VMEM(*entry) for entry in scratch]
         + [
             pltpu.SemaphoreType.DMA((9,)),
@@ -560,9 +574,9 @@
             jax.ShapeDtypeStruct((half * rows, width), F32),
             jax.ShapeDtypeStruct((1, 1), F32),
         ),
-        in_specs=[vmem, smem],
-        out_specs=(pl.BlockSpec(memory_space=pl.ANY), smem),
-        scratch_shapes=[pltpu.SemaphoreType.DMA],
+        in_specs=[vmem, vmem],
+        out_specs=(pl.BlockSpec(memory_space=pl.ANY), pl.BlockSpec(memory_space=pl.ANY)),
+        scratch_shapes=[pltpu.VMEM((1, 1), F32), pltpu.SemaphoreType.DMA((2,))],
         compiler_params=pltpu.CompilerParams(vmem_limit_bytes=1024 * 1024),
     )(gradient, cost)
     return gradient.reshape(increment.shape), cost.reshape(())

time: 33 us -> 31.2 us (0.945)
  Pallas kernels: 31.6 us -> 29.8 us
    pallas_call x1, Pallas kernels: 1.88 us -> 0.75 us  [body(): pl.pallas_call(deliver, out_shape=(jax.ShapeDtypeStruct((half * rows, wid...]
    pallas_call x1, Pallas kernels: 29.7 us -> 29 us  [body(): pl.pallas_call(functools.partial(kernel, (nlat, nlon, half, rows)), out_s...]
where the time goes in v4:
time: 31.2 us; the launch traced here: 31 us
  Pallas kernels  29.8 us (96%)
  between operations  1.29 us (4%)
    pallas_call x1, Pallas kernels, body(): pl.pallas_call(functools.partial(kernel, (nlat, nlon, half, rows)), out_s...  29 us
    pallas_call x1, Pallas kernels, body(): pl.pallas_call(deliver, out_shape=(jax.ShapeDtypeStruct((half * rows, wid...  0.75 us

profile of v4, /device:TPU:1, one launch (start us, length us, event | category | flops | bytes accessed | tf_op | source)
XLA Modules:
  0.0 31.0 jit_solution(364354275266370881)
XLA Ops:
  1.3 29.0 %shard_map.113 = (f32[640,128]{1,0:T(8,128)S(1)}, f32[1,128]{1,0:T(1,128)S(1)}) custom-call(f32[640,128]{1,0:T(8,128)} %bitcast.11, f32[640,128]{1,0:T(8,128)} %bitcast.12, f32[640,128]{1,0:T(8,128)} %bitcast.13, f32[1,40]{1,0:T(1,128)} %bitcast.16, f32[40,80]{1,0:T(8,128)} %mix_h.1, bf16[40,128]{1,0:T(8,128)(2,1)} %bitcast.14, f32[1,128]{1,0:T(1,128)} %bitcast.17, ...), custom_call_target="tpu_custom_call" | custom-call | tf_op jit(solution)/shard_map/pallas_call | solution.py:537
  30.3 0.7 %shard_map.114 = (f32[640,128]{1,0:T(8,128)}, f32[1,1]{1,0:T(1,128)}) custom-call(f32[640,128]{1,0:T(8,128)S(1)} %get-tuple-element.6.gradient, f32[1,128]{1,0:T(1,128)S(1)} %get-tuple-element.7.cost), custom_call_target="tpu_custom_call" | custom-call | tf_op jit(solution)/shard_map/pallas_call | solution.py:571

commit v5 on v4

--- a/solution.py
+++ b/solution.py
@@ -66,28 +66,35 @@
         loads[n].start()
 
     barrier = pltpu.get_barrier_semaphore()
-    senders = [(up, j, h), (down, j, h), (i, j, other)]
-    senders += [(a, side, k) for a in (i, up, down) for k in (0, 1)]
+    has_up, has_down = i < nlat - 1, i > 0
+
+    def signal(device):
+        pl.semaphore_signal(barrier, inc=1, device_id=device, device_id_type=MESH)
+
+    for device in [(i, j, other), (i, side, 0), (i, side, 1)]:
+        signal(device)
+
+    @pl.when(has_up)
+    def _():
+        for device in [(up, j, h), (up, side, 0), (up, side, 1)]:
+            signal(device)
+
+    @pl.when(has_down)
+    def _():
+        for device in [(down, j, h), (down, side, 0), (down, side, 1)]:
+            signal(device)
+
     ring = nlon // 2 if nlon % 2 == 0 else nlon
     laps = nlon // ring
     crowd = nlat * laps * 2
-    lap, place_in_ring = lax.div(j, ring), lax.rem(j, ring)
-    me = (i * laps + lap) * 2 + h
-
-    def companion(t):
-        index = lax.rem(me + t, crowd)
-        return (
-            lax.div(index, 2 * laps),
-            lax.rem(lax.div(index, 2), laps) * ring + place_in_ring,
-            lax.rem(index, 2),
-        )
-
-    def follower(t):
-        return (i, lap * ring + lax.rem(place_in_ring + t, ring), h)
-
-    senders += [companion(t) for t in range(1, crowd)] + [follower(t) for t in range(1, ring)]
-    for device in senders:
-        pl.semaphore_signal(barrier, inc=1, device_id=device, device_id_type=MESH)
+    lap = lax.div(j, ring)
+    latitudes = [lax.rem(i + k, nlat) for k in range(nlat)]
+    longitudes = [lax.rem(j + ring * k, nlon) for k in range(laps)]
+    companions = [(a, b, c) for a in latitudes for b in longitudes for c in (h, other)][1:]
+    followers = [(i, lap * ring + lax.rem(j - lap * ring + t, ring), h) for t in range(1, ring)]
+    for device in companions + followers:
+        signal(device)
+    arrivals = 3 + 3 * has_up.astype(jnp.int32) + 3 * has_down.astype(jnp.int32) + len(companions) + len(followers)
 
     def remote(n, source, target, device, arrival=None):
         return pltpu.make_async_remote_copy(
@@ -113,11 +120,34 @@
 
     pack(7)
     pack(0)
-    pl.semaphore_wait(barrier, len(senders))
+    pl.semaphore_wait(barrier, arrivals)
     near_s = remote(2, own.at[7], south.at[1], (up, j, h))
     near_n = remote(3, own.at[0], north.at[0], (down, j, h))
-    near_s.start()
-    near_n.start()
+
+    def launch(copies_up=(), copies_down=(), copies_both=()):
+        for condition, group in ((has_up, copies_up), (has_down, copies_down)):
+            if group:
+
+                @pl.when(condition)
+                def _(group=group):
+                    for copy in group:
+                        copy.start()
+
+        for copy in copies_both:
+            copy.start()
+
+    ups, downs, boths = [near_s], [near_n], []
+    launch([near_s], [near_n])
+
+    @pl.when(jnp.logical_not(has_down))
+    def _():
+        for ref in (south, south_in, strip_s, grid_s, edge_s):
+            ref[...] = jnp.zeros(ref.shape, ref.dtype)
+
+    @pl.when(jnp.logical_not(has_up))
+    def _():
+        for ref in (north, north_in, strip_n, grid_n, edge_n):
+            ref[...] = jnp.zeros(ref.shape, ref.dtype)
 
     wide = (32, 3 * LANES)
     number, lane = iota(wide, 0), iota(wide, 1)
@@ -139,16 +169,20 @@
         strip_e[g, :, 3 * half : LANES] = jnp.zeros((16, LANES - 3 * half), BF16)
         strip_w[g, :, 3 * half : LANES] = jnp.zeros((16, LANES - 3 * half), BF16)
 
-    copies = [
+    up_copies = [
         remote(8, strip_e.at[5], strip_s.at[h], (up, east, 0), 8 + h),
+        remote(10, strip_w.at[5], strip_s.at[h], (up, west, 1), 8 + h),
+    ]
+    down_copies = [
         remote(9, strip_e.at[0], strip_n.at[h], (down, east, 0), 10 + h),
-        remote(10, strip_w.at[5], strip_s.at[h], (up, west, 1), 8 + h),
         remote(11, strip_w.at[0], strip_n.at[h], (down, west, 1), 10 + h),
+    ]
+    side_copies = [
         remote(6, strip_e, strip_in.at[h], (i, east, 0), 6 + h),
         remote(7, strip_w, strip_in.at[h], (i, west, 1), 6 + h),
     ]
-    for copy in copies:
-        copy.start()
+    launch(up_copies, down_copies, side_copies)
+    ups, downs, boths = ups + up_copies, downs + down_copies, boths + side_copies
 
     for n in range(3, 8):
         loads[n].wait()
@@ -166,9 +200,8 @@
     far_s = remote(17, own.at[6], south.at[0], (up, j, h))
     far_n = remote(18, own.at[1], north.at[1], (down, j, h))
     own_copy.start()
-    far_s.start()
-    far_n.start()
-    copies += [near_s, near_n, misc_copy, own_copy, far_s, far_n]
+    launch([far_s], [far_n])
+    ups, downs, boths = ups + [far_s], downs + [far_n], boths + [misc_copy, own_copy]
 
     table = lut[...]
     low = dot_nt(one_hot(iota((LANES, LANES), 0) == iota((LANES, LANES), 1)), (table & 255).astype(F32).astype(BF16))
@@ -236,22 +269,17 @@
         block = jnp.concatenate([grid[:, at_row(4 * g + q)] for g in range(4)], axis=1)
         edge[:, 256 * q : 256 * q + depth] = dot_nt(outgoing, block).astype(BF16)
         edge[:, 256 * q + depth : 256 * (q + 1)] = jnp.zeros((16, 256 - depth), BF16)
-    late = [
+    late_up = [
         remote(12, grid.at[:, 14 * LANES : 16 * LANES], grid_s, (up, j, h)),
+        remote(15, edge.at[:, 768:1024], edge_s, (up, side, other)),
+    ]
+    late_down = [
         remote(13, grid.at[:, 0 : 2 * LANES], grid_n, (down, j, h)),
-        remote(14, edge, edge_in, (i, side, other)),
-        remote(15, edge.at[:, 768:1024], edge_s, (up, side, other)),
         remote(16, edge.at[:, 0:256], edge_n, (down, side, other)),
     ]
-    for copy in late:
-        copy.start()
-
-    near_s.wait_recv()
-    relays = [remote(4, south.at[1], south_in.at[1], (i, j, other))]
-    relays[0].start()
-    near_n.wait_recv()
-    relays.append(remote(5, north.at[0], north_in.at[0], (i, j, other)))
-    relays[1].start()
+    late_side = [remote(14, edge, edge_in, (i, side, other))]
+    launch(late_up, late_down, late_side)
+    ups, downs, boths = ups + late_up, downs + late_down, boths + late_side
 
     lane_row = iota((1, LANES), 1)
     patched = jnp.where(h == 0, lane_row - (LANES - HALO), HALO - 1 - lane_row) >= 0
@@ -285,9 +313,6 @@
     def patch_of(ref):
         return dot_tn(ref[:, 0 : 3 * half], place)
 
-    own_copy.wait_recv()
-    for k in (0, 1):
-        remote(6, strip_e, strip_in.at[k], (i, east, 0), 6 + k).wait_recv()
     group_of = {}
     for r in range(rows):
         g = max(n for n, start in enumerate(GROUPS) if start <= r and r < start + 3)
@@ -305,11 +330,34 @@
             found[g] = (patch_of(strip_in.at[h, g]), patch_of(strip_in.at[other, g]))
         return [value[half * t : half * (t + 1)] for value in found[g]]
 
+    own_copy.wait_recv()
     for q in range(rows // 2):
         mine, theirs = rows_of(own, q), rows_of(partner, q)
         for t in (0, 1):
-            r = 2 * q + t
-            assemble(HALO + r, (mine[t], theirs[t]), patches_for(r))
+            assemble(HALO + 2 * q + t, (mine[t], theirs[t]), (None, None))
+
+    def relay(arrived, condition, n, source, target):
+        copy = remote(n, source, target, (i, j, other))
+
+        @pl.when(condition)
+        def _():
+            arrived.wait_recv()
+            copy.start()
+
+        return copy
+
+    relays_s = [relay(near_s, has_down, 4, south.at[1], south_in.at[1])]
+    relays_n = [relay(near_n, has_up, 5, north.at[0], north_in.at[0])]
+
+    for k in (0, 1):
+        remote(6, strip_e, strip_in.at[k], (i, east, 0), 6 + k).wait_recv()
+    for r in range(rows):
+        patches = patches_for(r)
+        for f in range(3):
+            for span, patch in zip((here, there), patches):
+                current = targets[f][span, at_row(HALO + r)]
+                targets[f][span, at_row(HALO + r)] = jnp.where(patched, patch[:, at_row(f)], current)
+
     diffusion = full[2]
     centre = 1.0 - 4.0 * diffusion
 
@@ -379,11 +427,18 @@
         total = total + misfit(image_first(pair), pair, hold, 0)
         total = total + misfit(image_second(pair), pair, sm, 1)
 
-    for copy in relays:
-        copy.wait_recv()
-    for k in (0, 1):
-        remote(8, strip_e.at[5], strip_s.at[k], (i, east, 0), 8 + k).wait_recv()
-        remote(9, strip_e.at[0], strip_n.at[k], (i, east, 0), 10 + k).wait_recv()
+    @pl.when(has_down)
+    def _():
+        relays_s[0].wait_recv()
+        for k in (0, 1):
+            remote(8, strip_e.at[5], strip_s.at[k], (i, east, 0), 8 + k).wait_recv()
+
+    @pl.when(has_up)
+    def _():
+        relays_n[0].wait_recv()
+        for k in (0, 1):
+            remote(9, strip_e.at[0], strip_n.at[k], (i, east, 0), 10 + k).wait_recv()
+
     patch_s = (patch_of(strip_s.at[h]), patch_of(strip_s.at[other]))
     patch_n = (patch_of(strip_n.at[h]), patch_of(strip_n.at[other]))
 
@@ -408,18 +463,24 @@
         total = total + misfit(image_first(pair), pair, hold, 0)
         total = total + misfit(image_second(pair), pair, sm, 1)
     near[0] = known + 0.5 * jnp.sum(jnp.where(own_lanes, total, 0.0), axis=0, keepdims=True)
-    first_round = [remote(21 + t, near.at[0], near.at[t], companion(t)) for t in range(1, crowd)]
+    first_round = [remote(22, near.at[0], near.at[t + 1], device) for t, device in enumerate(companions)]
     for copy in first_round:
         copy.start()
 
-    far_s.wait_recv()
-    relays.append(remote(19, south.at[0], south_in.at[0], (i, j, other)))
-    relays[2].start()
-    far_n.wait_recv()
-    relays.append(remote(20, north.at[1], north_in.at[1], (i, j, other)))
-    relays[3].start()
-    for copy in late:
-        copy.wait_recv()
+    relays_s.append(relay(far_s, has_down, 19, south.at[0], south_in.at[0]))
+    relays_n.append(relay(far_n, has_up, 20, north.at[1], north_in.at[1]))
+    late_side[0].wait_recv()
+
+    @pl.when(has_down)
+    def _():
+        for copy in late_up:
+            copy.wait_recv()
+
+    @pl.when(has_up)
+    def _():
+        for copy in late_down:
+            copy.wait_recv()
+
     for q in range(4):
         value = dot_tn(edge_in[:, 256 * q : 256 * q + depth], incoming)
         for g in range(4):
@@ -432,8 +493,14 @@
     f1[:, at_row(18)] = jnp.where(patched, value[:, at_row(0)], grid_n[:, at_row(0)].astype(F32))
     f1[:, at_row(19)] = grid_n[:, at_row(1)].astype(F32)
 
-    for copy in relays[2:]:
-        copy.wait_recv()
+    @pl.when(has_down)
+    def _():
+        relays_s[1].wait_recv()
+
+    @pl.when(has_up)
+    def _():
+        relays_n[1].wait_recv()
+
     outer_rows(1)
     for pair in ((1, 2), (21, 22)):
         advance(pair)
@@ -464,13 +531,13 @@
     final = remote(21, back, back_in, (i, j, other))
     final.start()
 
-    for copy in first_round:
-        copy.wait_recv()
+    whole_first = remote(22, near.at[1:crowd], near.at[1:crowd], (i, j, other))
+    whole_first.wait_recv()
     part = near[0]
     for t in range(1, crowd):
         part = part + near[t]
     far[0] = part
-    second_round = [remote(21 + crowd + t, far.at[0], far.at[t], follower(t)) for t in range(1, ring)]
+    second_round = [remote(23, far.at[0], far.at[t + 1], device) for t, device in enumerate(followers)]
     for copy in second_round:
         copy.start()
 
@@ -481,15 +548,25 @@
             r = 2 * q + t
             adjoint = jnp.where(own_lanes, x1[here, at_row(r)], received[half * t : half * (t + 1)])
             out_ref[pl.ds(r, half, stride=rows), :] = inc[pl.ds(r, half, stride=rows), :] + adjoint
-    for copy in second_round:
-        copy.wait_recv()
+    whole_second = remote(23, far.at[1:ring], far.at[1:ring], (i, j, other))
+    whole_second.wait_recv()
     part = far[0]
     for t in range(1, ring):
         part = part + far[t]
     cells = full_levels * rows * LANES * nlat * nlon
     cost_ref[...] = jnp.broadcast_to(jnp.sum(part, axis=1, keepdims=True) * (1.0 / cells), (1, LANES))
-    for copy in copies + late + relays + [final] + first_round + second_round:
+    for copy in boths + [final, whole_first, whole_second]:
         copy.wait_send()
+
+    @pl.when(has_up)
+    def _():
+        for copy in ups + relays_n:
+            copy.wait_send()
+
+    @pl.when(has_down)
+    def _():
+        for copy in downs + relays_s:
+            copy.wait_send()
 
 
 def deliver(gradient, cost, gradient_out, cost_out, single, sem):
@@ -515,7 +592,7 @@
     grid_size = rows * width
     far = nlon // 2 if nlon % 2 == 0 else nlon
     near = nlat * (nlon // far) * 2
-    copies = 21 + near + far
+    copies = 24
     strip = (16, width)
     scratch = [
         ((half * rows, width), F32), ((half * rows, width), F32), ((half * rows, width), F32),

time: 31.2 us -> 30.2 us (0.968)
  Pallas kernels: 29.8 us -> 28.8 us
    pallas_call x1, Pallas kernels: 29 us -> 28 us  [body(): pl.pallas_call(functools.partial(kernel, (nlat, nlon, half, rows)), out_s...]
where the time goes in v5:
time: 30.2 us; the launch traced here: 30.1 us
  Pallas kernels  28.8 us (95%)
  between operations  1.29 us (4%)
    pallas_call x1, Pallas kernels, body(): pl.pallas_call(functools.partial(kernel, (nlat, nlon, half, rows)), out_s...  28 us
    pallas_call x1, Pallas kernels, body(): pl.pallas_call(deliver, out_shape=(jax.ShapeDtypeStruct((half * rows, wid...  0.75 us

profile of v5, /device:TPU:1, one launch (start us, length us, event | category | flops | bytes accessed | tf_op | source)
XLA Modules:
  0.0 30.1 jit_solution(9673876896948820641)
XLA Ops:
  1.3 28.0 %shard_map.113 = (f32[640,128]{1,0:T(8,128)S(1)}, f32[1,128]{1,0:T(1,128)S(1)}) custom-call(f32[640,128]{1,0:T(8,128)} %bitcast.11, f32[640,128]{1,0:T(8,128)} %bitcast.12, f32[640,128]{1,0:T(8,128)} %bitcast.13, f32[1,40]{1,0:T(1,128)} %bitcast.16, f32[40,80]{1,0:T(8,128)} %mix_h.1, bf16[40,128]{1,0:T(8,128)(2,1)} %bitcast.14, f32[1,128]{1,0:T(1,128)} %bitcast.17, ...), custom_call_target="tpu_custom_call" | custom-call | tf_op jit(solution)/shard_map/pallas_call | solution.py:614
  29.3 0.7 %shard_map.114 = (f32[640,128]{1,0:T(8,128)}, f32[1,1]{1,0:T(1,128)}) custom-call(f32[640,128]{1,0:T(8,128)S(1)} %get-tuple-element.6.gradient, f32[1,128]{1,0:T(1,128)S(1)} %get-tuple-element.7.cost), custom_call_target="tpu_custom_call" | custom-call | tf_op jit(solution)/shard_map/pallas_call | solution.py:648

commit v6 on v5

--- a/solution.py
+++ b/solution.py
@@ -45,10 +45,10 @@
     out_ref, cost_ref,
     inc, u, v, dif, mix, jac, w, y, lut,
     own, partner, misc, misc_in, full,
-    south, north, south_in, north_in,
+    halo_up, halo_down, south, north, south_in, north_in,
     strip_e, strip_w, strip_in, strip_s, strip_n,
     slots, pick, grid, grid_s, grid_n, edge, edge_in, edge_s, edge_n,
-    x0, x1, hu, hv, sm, f1, hold, back, back_in, near, far,
+    x0, x1, hu, hv, sm, f1, hold, back, back_in, near, far, far_sent,
     load_sem, send_sem, recv_sem,
 ):
     nlat, nlon, half, rows = sizes
@@ -87,14 +87,22 @@
     ring = nlon // 2 if nlon % 2 == 0 else nlon
     laps = nlon // ring
     crowd = nlat * laps * 2
+    leads, follows = h == 1, h == 0
     lap = lax.div(j, ring)
     latitudes = [lax.rem(i + k, nlat) for k in range(nlat)]
     longitudes = [lax.rem(j + ring * k, nlon) for k in range(laps)]
-    companions = [(a, b, c) for a in latitudes for b in longitudes for c in (h, other)][1:]
-    followers = [(i, lap * ring + lax.rem(j - lap * ring + t, ring), h) for t in range(1, ring)]
-    for device in companions + followers:
-        signal(device)
-    arrivals = 3 + 3 * has_up.astype(jnp.int32) + 3 * has_down.astype(jnp.int32) + len(companions) + len(followers)
+    plane = [(a, b) for a in latitudes for b in longitudes][1:]
+    line = [(i, lap * ring + lax.rem(j - lap * ring + t, ring)) for t in range(1, ring)]
+
+    @pl.when(leads)
+    def _():
+        for a, b in plane:
+            signal((a, b, 0))
+            signal((a, b, 1))
+
+    for a, b in line:
+        signal((a, b, 1))
+    arrivals = 3 + 3 * has_up.astype(jnp.int32) + 3 * has_down.astype(jnp.int32) + len(plane) + 2 * len(line) * h
 
     def remote(n, source, target, device, arrival=None):
         return pltpu.make_async_remote_copy(
@@ -118,11 +126,24 @@
         for f in range(3):
             own[q, f] = jnp.concatenate([own_row(f, 2 * q), own_row(f, 2 * q + 1)], axis=0).astype(BF16)
 
-    pack(7)
-    pack(0)
+    def halo_block(ref, n, first, second):
+        ref[n] = jnp.concatenate([own_row(*first), own_row(*second)], axis=0).astype(BF16)
+
+    def near_blocks(ref, order):
+        halo_block(ref, 0, (0, order[0]), (0, order[1]))
+        halo_block(ref, 1, (1, order[0]), (2, order[0]))
+
+    def far_blocks(ref, order):
+        halo_block(ref, 2, (0, order[2]), (0, order[3]))
+        halo_block(ref, 3, (1, order[1]), (2, order[1]))
+        halo_block(ref, 4, (1, order[2]), (2, order[2]))
+
+    top, bottom = tuple(range(rows - 1, rows - 5, -1)), (0, 1, 2, 3)
+    near_blocks(halo_up, top)
+    near_blocks(halo_down, bottom)
     pl.semaphore_wait(barrier, arrivals)
-    near_s = remote(2, own.at[7], south.at[1], (up, j, h))
-    near_n = remote(3, own.at[0], north.at[0], (down, j, h))
+    near_s = remote(2, halo_up.at[0:2], south.at[0:2], (up, j, h))
+    near_n = remote(3, halo_down.at[0:2], north.at[0:2], (down, j, h))
 
     def launch(copies_up=(), copies_down=(), copies_both=()):
         for condition, group in ((has_up, copies_up), (has_down, copies_down)):
@@ -194,11 +215,13 @@
     misc[2] = jnp.broadcast_to(column, (half, LANES))
     misc_copy = remote(1, misc, misc_in, (i, j, other))
     misc_copy.start()
-    for q in range(1, 7):
+    for q in range(rows // 2):
         pack(q)
+    far_blocks(halo_up, top)
+    far_blocks(halo_down, bottom)
     own_copy = remote(0, own, partner, (i, j, other))
-    far_s = remote(17, own.at[6], south.at[0], (up, j, h))
-    far_n = remote(18, own.at[1], north.at[1], (down, j, h))
+    far_s = remote(17, halo_up.at[2:5], south.at[2:5], (up, j, h))
+    far_n = remote(18, halo_down.at[2:5], north.at[2:5], (down, j, h))
     own_copy.start()
     launch([far_s], [far_n])
     ups, downs, boths = ups + [far_s], downs + [far_n], boths + [misc_copy, own_copy]
@@ -299,7 +322,7 @@
     targets = (x0, hu, hv)
 
     def assemble(e, sources, patches):
-        for f in range(3):
+        for f in range(len(sources[0])):
             for span, source, patch in zip((here, there), sources, patches):
                 value = source[f]
                 if patch is not None:
@@ -346,8 +369,8 @@
 
         return copy
 
-    relays_s = [relay(near_s, has_down, 4, south.at[1], south_in.at[1])]
-    relays_n = [relay(near_n, has_up, 5, north.at[0], north_in.at[0])]
+    relays_s = [relay(near_s, has_down, 4, south.at[0:2], south_in.at[0:2])]
+    relays_n = [relay(near_n, has_up, 5, north.at[0:2], north_in.at[0:2])]
 
     for k in (0, 1):
         remote(6, strip_e, strip_in.at[k], (i, east, 0), 6 + k).wait_recv()
@@ -442,19 +465,34 @@
     patch_s = (patch_of(strip_s.at[h]), patch_of(strip_s.at[other]))
     patch_n = (patch_of(strip_n.at[h]), patch_of(strip_n.at[other]))
 
+    def halo_rows(ref, which):
+        first = ref[2 * which].astype(F32)
+        winds = [ref[1 if which == 0 else 4].astype(F32), None]
+        return [
+            [first[half * t : half * (t + 1)]] + ([] if winds[t] is None else [winds[t][0:half], winds[t][half:]])
+            for t in (0, 1)
+        ]
+
     def outer_rows(which):
-        q = 1 - which
-        mine, theirs = rows_of(south, q), rows_of(south_in, q)
-        for t in (0, 1):
-            e = 2 * q + t
-            fit = [None if e == 0 else value[half * (e - 1) : half * e] for value in patch_s]
-            assemble(e, (mine[t], theirs[t]), fit)
-        q = which
-        mine, theirs = rows_of(north, q), rows_of(north_in, q)
-        for t in (0, 1):
-            e = 2 * q + t
-            fit = [None if e == 3 else value[half * e : half * (e + 1)] for value in patch_n]
-            assemble(HALO + rows + e, (mine[t], theirs[t]), fit)
+        for sign, edge_row, refs, patches in (
+            (-1, HALO - 1, (south, south_in), patch_s),
+            (1, HALO + rows, (north, north_in), patch_n),
+        ):
+            blocks = [halo_rows(ref, which) for ref in refs]
+            for t in (0, 1):
+                r = 2 * which + t
+                e = edge_row + sign * r
+                spot = 2 - r if sign < 0 else r
+                fit = [None if r == 3 else value[half * spot : half * (spot + 1)] for value in patches]
+                assemble(e, [block[t] for block in blocks], fit)
+            if which == 1:
+                winds = [ref[3].astype(F32) for ref in refs]
+                fit = [value[half : 2 * half] for value in patches]
+                e = edge_row + sign
+                for f in (1, 2):
+                    for span, wind, patch in zip((here, there), winds, fit):
+                        value = wind[half * (f - 1) : half * f]
+                        targets[f][span, at_row(e)] = keep(e, jnp.where(patched, patch[:, at_row(f)], value))
 
     outer_rows(0)
     for pair in ((3, 4), (19, 20)):
@@ -463,12 +501,17 @@
         total = total + misfit(image_first(pair), pair, hold, 0)
         total = total + misfit(image_second(pair), pair, sm, 1)
     near[0] = known + 0.5 * jnp.sum(jnp.where(own_lanes, total, 0.0), axis=0, keepdims=True)
-    first_round = [remote(22, near.at[0], near.at[t + 1], device) for t, device in enumerate(companions)]
+    own_part = remote(22, near.at[0], near.at[1], (i, j, 1))
+    first_round = [remote(22, near.at[0], near.at[2 + 2 * t + h], (a, b, 1)) for t, (a, b) in enumerate(plane)]
     for copy in first_round:
         copy.start()
 
-    relays_s.append(relay(far_s, has_down, 19, south.at[0], south_in.at[0]))
-    relays_n.append(relay(far_n, has_up, 20, north.at[1], north_in.at[1]))
+    @pl.when(follows)
+    def _():
+        own_part.start()
+
+    relays_s.append(relay(far_s, has_down, 19, south.at[2:5], south_in.at[2:5]))
+    relays_n.append(relay(far_n, has_up, 20, north.at[2:5], north_in.at[2:5]))
     late_side[0].wait_recv()
 
     @pl.when(has_down)
@@ -532,14 +575,20 @@
     final.start()
 
     whole_first = remote(22, near.at[1:crowd], near.at[1:crowd], (i, j, other))
-    whole_first.wait_recv()
-    part = near[0]
-    for t in range(1, crowd):
-        part = part + near[t]
-    far[0] = part
-    second_round = [remote(23, far.at[0], far.at[t + 1], device) for t, device in enumerate(followers)]
-    for copy in second_round:
-        copy.start()
+    sent_first = remote(22, near.at[1 : crowd // 2], near.at[1 : crowd // 2], (i, j, other))
+    second_round = [remote(23, far.at[0], far.at[t + 1], (a, b, c)) for t, (a, b) in enumerate(line) for c in (0, 1)]
+    handed = remote(24, far.at[0], far.at[ring], (i, j, 0))
+
+    @pl.when(leads)
+    def _():
+        whole_first.wait_recv()
+        part = near[0]
+        for t in range(1, crowd):
+            part = part + near[t]
+        far[0] = part
+        for copy in second_round:
+            copy.start()
+        handed.start()
 
     final.wait_recv()
     for q in range(rows // 2):
@@ -549,14 +598,30 @@
             adjoint = jnp.where(own_lanes, x1[here, at_row(r)], received[half * t : half * (t + 1)])
             out_ref[pl.ds(r, half, stride=rows), :] = inc[pl.ds(r, half, stride=rows), :] + adjoint
     whole_second = remote(23, far.at[1:ring], far.at[1:ring], (i, j, other))
+    sent_second = remote(23, far_sent, far_sent, (i, j, other))
     whole_second.wait_recv()
+
+    @pl.when(follows)
+    def _():
+        handed.wait_recv()
+        far[0] = far[ring]
+
     part = far[0]
     for t in range(1, ring):
         part = part + far[t]
     cells = full_levels * rows * LANES * nlat * nlon
     cost_ref[...] = jnp.broadcast_to(jnp.sum(part, axis=1, keepdims=True) * (1.0 / cells), (1, LANES))
-    for copy in boths + [final, whole_first, whole_second]:
+    for copy in boths + [final, sent_first]:
         copy.wait_send()
+
+    @pl.when(follows)
+    def _():
+        own_part.wait_send()
+
+    @pl.when(leads)
+    def _():
+        sent_second.wait_send()
+        handed.wait_send()
 
     @pl.when(has_up)
     def _():
@@ -592,7 +657,7 @@
     grid_size = rows * width
     far = nlon // 2 if nlon % 2 == 0 else nlon
     near = nlat * (nlon // far) * 2
-    copies = 24
+    copies = 25
     strip = (16, width)
     scratch = [
         ((half * rows, width), F32), ((half * rows, width), F32), ((half * rows, width), F32),
@@ -600,8 +665,7 @@
         ((32, channels, width), BF16), ((16, width), jnp.int32),
         ((8, 3, levels, width), BF16), ((8, 3, levels, width), BF16),
         ((3, half, width), F32), ((3, half, width), F32), ((3, levels, width), F32),
-        ((2, 3, levels, width), BF16), ((2, 3, levels, width), BF16),
-        ((2, 3, levels, width), BF16), ((2, 3, levels, width), BF16),
+        *[((5, levels, width), BF16)] * 6,
         ((6, *strip), BF16), ((6, *strip), BF16), ((2, 6, *strip), BF16), ((2, *strip), BF16), ((2, *strip), BF16),
         ((depth, grid_size), BF16), ((grid_size, 2 * width), BF16), ((depth, grid_size), BF16),
         ((depth, 2 * width), BF16), ((depth, 2 * width), BF16),
@@ -609,7 +673,7 @@
         ((levels, wide), F32), ((levels, wide), F32), ((levels, wide), F32), ((levels, wide), F32), ((levels, wide), F32),
         ((depth, 20 * width), F32),
         ((levels, wide), F32), ((8, levels, width), BF16), ((8, levels, width), BF16),
-        ((near, 1, width), F32), ((far, 1, width), F32),
+        ((near, 1, width), F32), ((far + 1, 1, width), F32), ((2 * far - 2, 1, width), F32),
     ]
     gradient, cost = pl.pallas_call(
         functools.partial(kernel, (nlat, nlon, half, rows)),

time: 30.2 us -> 29 us (0.960)
  Pallas kernels: 28.8 us -> 27.6 us
    pallas_call x1, Pallas kernels: 28 us -> 26.8 us  [body(): pl.pallas_call(functools.partial(kernel, (nlat, nlon, half, rows)), out_s...]
where the time goes in v6:
time: 29 us; the launch traced here: 28.8 us
  Pallas kernels  27.6 us (95%)
  between operations  1.29 us (4%)
    pallas_call x1, Pallas kernels, body(): pl.pallas_call(functools.partial(kernel, (nlat, nlon, half, rows)), out_s...  26.8 us
    pallas_call x1, Pallas kernels, body(): pl.pallas_call(deliver, out_shape=(jax.ShapeDtypeStruct((half * rows, wid...  0.75 us

profile of v6, /device:TPU:1, one launch (start us, length us, event | category | flops | bytes accessed | tf_op | source)
XLA Modules:
  0.0 28.8 jit_solution(13367901981911321084)
XLA Ops:
  1.3 26.8 %shard_map.113 = (f32[640,128]{1,0:T(8,128)S(1)}, f32[1,128]{1,0:T(1,128)S(1)}) custom-call(f32[640,128]{1,0:T(8,128)} %bitcast.11, f32[640,128]{1,0:T(8,128)} %bitcast.12, f32[640,128]{1,0:T(8,128)} %bitcast.13, f32[1,40]{1,0:T(1,128)} %bitcast.16, f32[40,80]{1,0:T(8,128)} %mix_h.1, bf16[40,128]{1,0:T(8,128)(2,1)} %bitcast.14, f32[1,128]{1,0:T(1,128)} %bitcast.17, ...), custom_call_target="tpu_custom_call" | custom-call | tf_op jit(solution)/shard_map/pallas_call | solution.py:678
  28.1 0.7 %shard_map.114 = (f32[640,128]{1,0:T(8,128)}, f32[1,1]{1,0:T(1,128)}) custom-call(f32[640,128]{1,0:T(8,128)S(1)} %get-tuple-element.6.gradient, f32[1,128]{1,0:T(1,128)S(1)} %get-tuple-element.7.cost), custom_call_target="tpu_custom_call" | custom-call | tf_op jit(solution)/shard_map/pallas_call | solution.py:712

commit v7 on v6

--- a/solution.py
+++ b/solution.py
@@ -241,14 +241,14 @@
         jnp.where(iota((LANES, LANES), 0) == iota((LANES, LANES), 1), w_row, 0.0), axis=1, keepdims=True
     )
     squares = jnp.zeros((LANES, LANES), F32)
-    for s in range(16):
-        first, second = y[s].astype(F32), y[16 + s].astype(F32)
-        squares = squares + live[s] * (first * first + second * second)
+    for s in range(8):
+        first, second = y[8 * h + s].astype(F32), y[16 + 8 * h + s].astype(F32)
+        squares = squares + jnp.where(count > 8 * h + s, 1.0, 0.0) * (first * first + second * second)
     squares = squares * w_column
 
     increment = inc[...]
     known = 0.5 * jnp.sum(increment * increment, axis=0, keepdims=True)
-    known = known + 0.25 * jnp.sum(squares, axis=0, keepdims=True)
+    known = known + 0.5 * jnp.sum(squares, axis=0, keepdims=True)
 
     misc_copy.wait_recv()
     here, there = pl.ds(pl.multiple_of(h * half, 8), half), pl.ds(pl.multiple_of(other * half, 8), half)
@@ -261,8 +261,8 @@
     jac_t = full[1].astype(BF16)
     weighted = (full[1] * w_row).astype(BF16)
     gram_full = dot_nt(weighted, jac_t)
-    gram = gram_full.astype(BF16)
-    gram = jnp.concatenate([gram, (gram_full - gram.astype(F32)).astype(BF16)], axis=1)
+    image_matrix = gram_full + dot(gram_full.astype(BF16), mixing)
+    both = jnp.concatenate([mixing, image_matrix.astype(BF16)], axis=0)
 
     for s in range(16):
         span = slice(LANES * s, LANES * (s + 1))
@@ -271,8 +271,8 @@
         slots[:, span] = jnp.concatenate(
             [first, second, jnp.broadcast_to(live[s], (16, LANES))], axis=0
         ).astype(BF16)
-    for q in range(rows // 2):
-        masked = jnp.concatenate(
+    def masked(q):
+        return jnp.concatenate(
             [
                 slots[:, LANES * s : LANES * (s + 1)]
                 * jnp.broadcast_to(jnp.where(pair_of[s : s + 1, :] == q, 1.0, 0.0), (slots.shape[0], LANES)).astype(BF16)
@@ -280,7 +280,11 @@
             ],
             axis=1,
         )
-        grid[:, 2 * LANES * q : 2 * LANES * (q + 1)] = dot(masked, pick[...]).astype(BF16)
+
+    for q in range(0, rows // 2, 2):
+        moved = dot(jnp.concatenate([masked(q), masked(q + 1)], axis=0), pick[...]).astype(BF16)
+        for t in (0, 1):
+            grid[:, 2 * LANES * (q + t) : 2 * LANES * (q + t + 1)] = moved[slots.shape[0] * t : slots.shape[0] * (t + 1)]
 
     def edge_selector(core):
         number, lane = iota((16, 4 * LANES), 0), iota((16, 4 * LANES), 1)
@@ -415,40 +419,38 @@
     def pairwise(first, last):
         return [tuple(range(e, min(e + 2, last + 1))) for e in range(first, last + 1, 2)]
 
+    def both_of(pair, source, target):
+        values = [step_row(source, e) for e in pair]
+        joined = jnp.concatenate(values, axis=1).astype(BF16)
+        result = dot(both, joined)
+        for n, e in enumerate(pair):
+            target[:, at_row(e)] = result[full_levels:, at_row(n)]
+        return [value + result[0:full_levels, at_row(n)] for n, value in enumerate(values)]
+
+    def misfit(states, pair, target, step):
+        parts = []
+        for state, e in zip(states, pair):
+            r = e - HALO
+            if 0 <= r < rows:
+                moved = grid[full_levels * step : full_levels * (step + 1), at_row(r)].astype(F32)
+                alive = grid[2 * full_levels : depth, at_row(r)].astype(F32)[0:1]
+                parts.append(state * (alive * target[:, at_row(e)] - 2.0 * moved))
+        return sum(parts)
+
     def advance(pair):
-        values = coupled(mixing, [step_row(x0, e) for e in pair])
-        for e, value in zip(pair, values):
+        states = both_of(pair, x0, hold)
+        for e, value in zip(pair, states):
             x1[:, at_row(e)] = keep(e, value)
-
-    def image_of(states, pair, target):
-        halves = [state.astype(BF16) for state in states]
-        joined = jnp.concatenate(halves, axis=1)
-        image = dot(gram, jnp.concatenate([joined, joined], axis=0))
-        for n, e in enumerate(pair):
-            target[:, at_row(e)] = image[:, at_row(n)]
-        return halves
-
-    def misfit(halves, pair, target, step):
-        parts = []
-        for half_state, e in zip(halves, pair):
-            r = e - HALO
-            moved = grid[full_levels * step : full_levels * (step + 1), at_row(r)].astype(F32)
-            alive = grid[2 * full_levels : depth, at_row(r)].astype(F32)[0:1]
-            parts.append(half_state.astype(F32) * (alive * target[:, at_row(e)] - 2.0 * moved))
-        return sum(parts)
-
-    def image_first(pair):
-        return image_of([x1[:, at_row(e)] for e in pair], pair, hold)
-
-    def image_second(pair):
-        return image_of(coupled(mixing, [step_row(x1, e) for e in pair]), pair, sm)
-
+        return misfit(states, pair, hold, 0)
+
+    def advance_second(pair):
+        return misfit(both_of(pair, x1, sm), pair, sm, 1)
+
+    total = jnp.zeros((full_levels, LANES), F32)
     for pair in pairwise(5, 18):
-        advance(pair)
-    total = jnp.zeros((full_levels, LANES), F32)
+        total = total + advance(pair)
     for pair in pairwise(6, 17):
-        total = total + misfit(image_first(pair), pair, hold, 0)
-        total = total + misfit(image_second(pair), pair, sm, 1)
+        total = total + advance_second(pair)
 
     @pl.when(has_down)
     def _():
@@ -496,10 +498,9 @@
 
     outer_rows(0)
     for pair in ((3, 4), (19, 20)):
-        advance(pair)
+        total = total + advance(pair)
     for pair in ((4, 5), (18, 19)):
-        total = total + misfit(image_first(pair), pair, hold, 0)
-        total = total + misfit(image_second(pair), pair, sm, 1)
+        total = total + advance_second(pair)
     near[0] = known + 0.5 * jnp.sum(jnp.where(own_lanes, total, 0.0), axis=0, keepdims=True)
     own_part = remote(22, near.at[0], near.at[1], (i, j, 1))
     first_round = [remote(22, near.at[0], near.at[2 + 2 * t + h], (a, b, 1)) for t, (a, b) in enumerate(plane)]
@@ -547,10 +548,8 @@
     outer_rows(1)
     for pair in ((1, 2), (21, 22)):
         advance(pair)
-    for pair in ((3,), (20,)):
-        image_first(pair)
     for pair in ((2, 3), (20, 21)):
-        image_second(pair)
+        advance_second(pair)
 
     def force(e, target, step):
         moved = f1[full_levels * step : full_levels * (step + 1), at_row(e - 2)]

time: 29 us -> 28.1 us (0.969)
  Pallas kernels: 27.6 us -> 26.7 us
    pallas_call x1, Pallas kernels: 26.8 us -> 26 us  [body(): pl.pallas_call(functools.partial(kernel, (nlat, nlon, half, rows)), out_s...]
where the time goes in v7:
time: 28.1 us; the launch traced here: 28 us
  Pallas kernels  26.7 us (95%)
  between operations  1.29 us (5%)
    pallas_call x1, Pallas kernels, body(): pl.pallas_call(functools.partial(kernel, (nlat, nlon, half, rows)), out_s...  26 us
    pallas_call x1, Pallas kernels, body(): pl.pallas_call(deliver, out_shape=(jax.ShapeDtypeStruct((half * rows, wid...  0.75 us

profile of v7, /device:TPU:1, one launch (start us, length us, event | category | flops | bytes accessed | tf_op | source)
XLA Modules:
  0.0 28.0 jit_solution(9037572473281502888)
XLA Ops:
  1.3 26.0 %shard_map.113 = (f32[640,128]{1,0:T(8,128)S(1)}, f32[1,128]{1,0:T(1,128)S(1)}) custom-call(f32[640,128]{1,0:T(8,128)} %bitcast.11, f32[640,128]{1,0:T(8,128)} %bitcast.12, f32[640,128]{1,0:T(8,128)} %bitcast.13, f32[1,40]{1,0:T(1,128)} %bitcast.16, f32[40,80]{1,0:T(8,128)} %mix_h.1, bf16[40,128]{1,0:T(8,128)(2,1)} %bitcast.14, f32[1,128]{1,0:T(1,128)} %bitcast.17, ...), custom_call_target="tpu_custom_call" | custom-call | tf_op jit(solution)/shard_map/pallas_call | solution.py:677
  27.3 0.7 %shard_map.114 = (f32[640,128]{1,0:T(8,128)}, f32[1,1]{1,0:T(1,128)}) custom-call(f32[640,128]{1,0:T(8,128)S(1)} %get-tuple-element.6.gradient, f32[1,128]{1,0:T(1,128)S(1)} %get-tuple-element.7.cost), custom_call_target="tpu_custom_call" | custom-call | tf_op jit(solution)/shard_map/pallas_call | solution.py:711

commit v8 on v7

--- a/solution.py
+++ b/solution.py
@@ -272,14 +272,12 @@
             [first, second, jnp.broadcast_to(live[s], (16, LANES))], axis=0
         ).astype(BF16)
     def masked(q):
-        return jnp.concatenate(
-            [
-                slots[:, LANES * s : LANES * (s + 1)]
-                * jnp.broadcast_to(jnp.where(pair_of[s : s + 1, :] == q, 1.0, 0.0), (slots.shape[0], LANES)).astype(BF16)
-                for s in range(16)
-            ],
-            axis=1,
-        )
+        pieces = []
+        for s in range(16):
+            match = jnp.broadcast_to(jnp.where(pair_of[s : s + 1, :] == q, 1.0, 0.0), (16, LANES)).astype(BF16)
+            tiles = slots[:, LANES * s : LANES * (s + 1)].reshape(slots.shape[0] // 16, 16, LANES)
+            pieces.append((tiles * match[None]).reshape(slots.shape[0], LANES))
+        return jnp.concatenate(pieces, axis=1)
 
     for q in range(0, rows // 2, 2):
         moved = dot(jnp.concatenate([masked(q), masked(q + 1)], axis=0), pick[...]).astype(BF16)
@@ -504,8 +502,8 @@
     near[0] = known + 0.5 * jnp.sum(jnp.where(own_lanes, total, 0.0), axis=0, keepdims=True)
     own_part = remote(22, near.at[0], near.at[1], (i, j, 1))
     first_round = [remote(22, near.at[0], near.at[2 + 2 * t + h], (a, b, 1)) for t, (a, b) in enumerate(plane)]
-    for copy in first_round:
-        copy.start()
+    for t in sorted(range(len(plane)), key=lambda t: -min(t // laps + 1, nlat - t // laps - 1)):
+        first_round[t].start()
 
     @pl.when(follows)
     def _():
@@ -566,28 +564,28 @@
         for e, value in zip(pair, coupled(mixing_back, values)):
             sm[:, at_row(e)] = keep(e, value)
 
+    whole_first = remote(22, near.at[1:crowd], near.at[1:crowd], (i, j, other))
+    sent_first = remote(22, near.at[1 : crowd // 2], near.at[1 : crowd // 2], (i, j, other))
+    second_round = [remote(23, far.at[0], far.at[t + 1], (a, b, c)) for t, (a, b) in enumerate(line) for c in (0, 1)]
+    handed = remote(24, far.at[0], far.at[ring], (i, j, 0))
+
+    @pl.when(leads)
+    def _():
+        whole_first.wait_recv()
+        part = near[0]
+        for t in range(1, crowd):
+            part = part + near[t]
+        far[0] = part
+        for t in sorted(range(len(second_round)), key=lambda t: -min(t // 2 + 1, ring - t // 2 - 1)):
+            second_round[t].start()
+        handed.start()
+
     for r in range(rows):
         x1[:, at_row(r)] = back_row(sm, r + HALO)
     for q in range(rows // 2):
         back[q] = jnp.concatenate([x1[there, at_row(2 * q)], x1[there, at_row(2 * q + 1)]], axis=0).astype(BF16)
     final = remote(21, back, back_in, (i, j, other))
     final.start()
-
-    whole_first = remote(22, near.at[1:crowd], near.at[1:crowd], (i, j, other))
-    sent_first = remote(22, near.at[1 : crowd // 2], near.at[1 : crowd // 2], (i, j, other))
-    second_round = [remote(23, far.at[0], far.at[t + 1], (a, b, c)) for t, (a, b) in enumerate(line) for c in (0, 1)]
-    handed = remote(24, far.at[0], far.at[ring], (i, j, 0))
-
-    @pl.when(leads)
-    def _():
-        whole_first.wait_recv()
-        part = near[0]
-        for t in range(1, crowd):
-            part = part + near[t]
-        far[0] = part
-        for copy in second_round:
-            copy.start()
-        handed.start()
 
     final.wait_recv()
     for q in range(rows // 2):

time: 28.1 us -> 28.1 us (level)
  no operation moved by 1% of the time
where the time goes in v8:
time: 28.1 us; the launch traced here: 28 us
  Pallas kernels  26.7 us (95%)
  between operations  1.29 us (5%)
    pallas_call x1, Pallas kernels, body(): pl.pallas_call(functools.partial(kernel, (nlat, nlon, half, rows)), out_s...  25.9 us
    pallas_call x1, Pallas kernels, body(): pl.pallas_call(deliver, out_shape=(jax.ShapeDtypeStruct((half * rows, wid...  0.75 us

profile of v8, /device:TPU:1, one launch (start us, length us, event | category | flops | bytes accessed | tf_op | source)
XLA Modules:
  0.0 28.0 jit_solution(12364481622049913399)
XLA Ops:
  1.3 25.9 %shard_map.113 = (f32[640,128]{1,0:T(8,128)S(1)}, f32[1,128]{1,0:T(1,128)S(1)}) custom-call(f32[640,128]{1,0:T(8,128)} %bitcast.11, f32[640,128]{1,0:T(8,128)} %bitcast.12, f32[640,128]{1,0:T(8,128)} %bitcast.13, f32[1,40]{1,0:T(1,128)} %bitcast.16, f32[40,80]{1,0:T(8,128)} %mix_h.1, bf16[40,128]{1,0:T(8,128)(2,1)} %bitcast.14, f32[1,128]{1,0:T(1,128)} %bitcast.17, ...), custom_call_target="tpu_custom_call" | custom-call | tf_op jit(solution)/shard_map/pallas_call | solution.py:675
  27.2 0.7 %shard_map.114 = (f32[640,128]{1,0:T(8,128)}, f32[1,1]{1,0:T(1,128)}) custom-call(f32[640,128]{1,0:T(8,128)S(1)} %get-tuple-element.6.gradient, f32[1,128]{1,0:T(1,128)S(1)} %get-tuple-element.7.cost), custom_call_target="tpu_custom_call" | custom-call | tf_op jit(solution)/shard_map/pallas_call | solution.py:709
